TPU v7x, 32 devices: a whole 2x2x4 slice. The times are simulated.
32 devices in a mesh: branch: 4 (over z), row: 4 (over y, core), col: 2 (over x).
Axes of the slice: x: 2, y: 2, z: 4, core: 2. Of those that a mesh axis runs over, the one named last changes fastest.
Arguments:
- homolog_tensor: bfloat16 [64, 128, 256], P('col', 'row'), may hold values from -6 to 6
- couple_tensor: bfloat16 [128, 128, 128], P('row', 'col'), may hold values from -6 to 6
- probe_matrix: bfloat16 [256, 256], P(None, 'branch'), may hold values from -0.375 to 0.375
- lookup_matrix: bfloat16 [256, 256], P(None, 'branch'), may hold values from -0.375 to 0.375
- content_matrix: bfloat16 [256, 256], P(None, 'branch'), may hold values from -0.375 to 0.375
- scoring_sigmoid_matrix: bfloat16 [256, 256], P(None, 'branch'), may hold values from -0.375 to 0.375
- scoring_final_matrix: bfloat16 [256, 256], P('branch'), may hold values from -0.375 to 0.375
- couple_offset_matrix: bfloat16 [128, 8], P(None, 'branch'), may hold values from -43 to 43
- product_first_matrix: bfloat16 [256, 32], replicated, may hold values from -0.375 to 0.375
- product_second_matrix: bfloat16 [256, 32], replicated, may hold values from -0.375 to 0.375
- product_final_matrix: bfloat16 [1024, 128], replicated, may hold values from -1 to 1
- trio_first_matrix: bfloat16 [2, 128, 128], P(None, None, 'branch'), may hold values from -0.5 to 0.5
- trio_second_matrix: bfloat16 [2, 128, 128], P(None, None, 'branch'), may hold values from -0.5 to 0.5
- trio_sigmoid_matrix: bfloat16 [128, 128], replicated, may hold values from -0.5 to 0.5
- trio_final_matrix: bfloat16 [128, 128], replicated, may hold values from -0.5 to 0.5
Outputs:
- revised_homolog_matrix: bfloat16 [64, 128, 256], P('col', 'row', 'branch')
- pairwise_output: bfloat16 [128, 128, 128], P('row', 'col')
All inputs are finite; a program needn't handle non-finite values.
Results may differ from a plain program's by a relative error of at most 0.014.
Values may be sent and summed in bfloat16 or wider, within the bound.
No kernel may reach another device: no remote copies, remote signals or barrier semaphores. Data moves between devices by JAX's collectives and lax.ppermute only.
A program may use at most 64 MiB of HBM per device.

v0:
```python
import functools

import jax
import jax.numpy as jnp
from jax import lax
from jax.experimental import pallas as pl
from jax.experimental.pallas import tpu as pltpu
from jax.sharding import PartitionSpec as P


EPS = 1e-05


def spread_2(block, axis, owner):
    block = jnp.where(lax.axis_index(axis) == owner, block, jnp.zeros_like(block))
    return lax.psum(block, axis)


def standardise_rows(values):
    values = values.astype(jnp.float32)
    centred = values - jnp.mean(values, axis=-1, keepdims=True)
    variance = jnp.mean(centred * centred, axis=-1, keepdims=True)
    return centred / jnp.sqrt(variance + EPS)


def apply_linear(source, weights):
    return jnp.dot(
        source.reshape(-1, weights.shape[0]), weights, preferred_element_type=jnp.float32
    )


def attend(query, key, value, bias):
    scale = float(query.shape[-1]) ** (-0.5)
    scores = jnp.einsum("sihd,sjhd->shij", query, key, preferred_element_type=jnp.float32) * scale
    scores = scores + jnp.transpose(bias, (2, 0, 1)).astype(jnp.float32)[None]
    top = jnp.max(scores, axis=-1, keepdims=True)
    expo = jnp.exp(scores - top)
    total = jnp.sum(expo, axis=-1)
    summed = jnp.einsum(
        "shij,sjhd->sihd", expo.astype(jnp.bfloat16), value, preferred_element_type=jnp.float32
    )
    return summed / jnp.transpose(total, (0, 2, 1))[..., None]


def plain_per_device(
    homolog_tensor,
    couple_tensor,
    probe_matrix,
    lookup_matrix,
    content_matrix,
    scoring_sigmoid_matrix,
    scoring_final_matrix,
    couple_offset_matrix,
    product_first_matrix,
    product_second_matrix,
    product_final_matrix,
    trio_first_matrix,
    trio_second_matrix,
    trio_sigmoid_matrix,
    trio_final_matrix,
):
    branches = lax.axis_size("branch")
    rows_count = lax.axis_size("row")
    cols_count = lax.axis_size("col")
    quadrant_share = lax.axis_index("branch")
    col_index = lax.axis_index("col")
    homolog_share, position_tile, channel_extent = homolog_tensor.shape
    c_block = couple_tensor.shape[1]
    residues = position_tile * rows_count
    depth = probe_matrix.shape[1]
    local_heads = couple_offset_matrix.shape[1]
    head_size = depth // local_heads
    q_rows = position_tile // branches
    total_rows = homolog_share * cols_count
    outer_width = product_first_matrix.shape[1]
    standardised_tensor = standardise_rows(homolog_tensor).astype(jnp.bfloat16)
    pair_normed = standardise_rows(couple_tensor).astype(jnp.bfloat16)
    bias_tile = (
        apply_linear(pair_normed, couple_offset_matrix)
        .astype(jnp.bfloat16)
        .reshape(position_tile, c_block, local_heads)
    )
    bias_band = lax.all_gather(bias_tile, "col", axis=1, tiled=True)
    spread = lax.all_to_all(standardised_tensor, "row", split_axis=0, concat_axis=1, tiled=True)
    few = spread.shape[0]
    shaped = (few, residues, local_heads, head_size)
    query = apply_linear(spread, probe_matrix).astype(jnp.bfloat16).reshape(shaped)
    key = apply_linear(spread, lookup_matrix).astype(jnp.bfloat16).reshape(shaped)
    value = apply_linear(spread, content_matrix).astype(jnp.bfloat16).reshape(shaped)
    gate_pre = apply_linear(spread, scoring_sigmoid_matrix).reshape(shaped)
    bias_full = lax.all_gather(bias_band, "row", axis=0, tiled=True)
    attended_values = attend(query, key, value, bias_full) * jax.nn.sigmoid(gate_pre)
    attended_values = attended_values.astype(jnp.bfloat16).reshape(few, residues, depth)
    attended_values = lax.all_to_all(
        attended_values, "row", split_axis=1, concat_axis=0, tiled=True
    )
    joined_tensor = apply_linear(attended_values, scoring_final_matrix).reshape(
        homolog_share, position_tile, channel_extent
    )
    joined_tensor = lax.psum_scatter(
        joined_tensor.astype(jnp.bfloat16), "branch", scatter_dimension=2, tiled=True
    ).astype(jnp.float32)
    device_share = channel_extent // branches
    local_alignment = lax.dynamic_slice_in_dim(
        homolog_tensor, quadrant_share * device_share, device_share, 2
    )
    revised_homolog_matrix = (local_alignment.astype(jnp.float32) + joined_tensor).astype(
        jnp.bfloat16
    )
    left_rows = lax.dynamic_slice_in_dim(standardised_tensor, quadrant_share * q_rows, q_rows, 1)
    left_outer = (
        apply_linear(left_rows, product_first_matrix)
        .astype(jnp.bfloat16)
        .reshape(homolog_share, q_rows * outer_width)
    )
    right_local = (
        apply_linear(standardised_tensor, product_second_matrix)
        .astype(jnp.bfloat16)
        .reshape(homolog_share, position_tile, outer_width)
    )
    right_outer = lax.all_gather(right_local, "row", axis=1, tiled=True)
    wide_out = product_final_matrix.astype(jnp.float32)
    left_major = jnp.transpose(left_outer)
    count = lax.axis_size("col") * c_block
    piece = right_outer.reshape(homolog_share, count * outer_width)
    outer = jnp.dot(left_major, piece, preferred_element_type=jnp.float32)
    outer = outer.reshape(q_rows, outer_width, count, outer_width)
    outer = jnp.transpose(outer, (2, 0, 1, 3)).reshape(count * q_rows, outer_width * outer_width)
    term = jnp.dot(outer, wide_out, precision=lax.Precision.HIGHEST) / total_rows
    update = lax.psum_scatter(
        term.reshape(count, q_rows, wide_out.shape[1]).astype(jnp.bfloat16),
        "col",
        scatter_dimension=0,
        tiled=True,
    ).astype(jnp.float32)
    update = jnp.transpose(update, (1, 0, 2))
    pair_rows = lax.dynamic_slice_in_dim(couple_tensor, quadrant_share * q_rows, q_rows, 0)
    mid_rows = (pair_rows.astype(jnp.float32) + update).astype(jnp.bfloat16)
    pair_mid = lax.all_gather(mid_rows, "branch", axis=0, tiled=True)
    tri_normed = standardise_rows(pair_mid).astype(jnp.bfloat16)

    def gated(weights):
        linear = apply_linear(tri_normed, weights[0])
        opening = apply_linear(tri_normed, weights[1])
        return (
            (jax.nn.sigmoid(opening) * linear)
            .astype(jnp.bfloat16)
            .reshape(position_tile, c_block, weights.shape[2])
        )

    tri_left = gated(trio_first_matrix)
    tri_right = gated(trio_second_matrix)
    left_band, right_band = (
        lax.all_gather(tri_left, "col", axis=1, tiled=True),
        lax.all_gather(tri_right, "col", axis=1, tiled=True),
    )
    ratio = rows_count // cols_count

    def mirror(offset):
        return spread_2(right_band, "row", col_index * ratio + offset)

    right_cols = jnp.concatenate([mirror(offset) for offset in range(ratio)], axis=0)
    product = jnp.einsum("ikc,jkc->ijc", left_band, right_cols, preferred_element_type=jnp.float32)
    product = lax.all_to_all(product, "branch", split_axis=0, concat_axis=2, tiled=True)
    product_normed = standardise_rows(product).astype(jnp.bfloat16)
    own_normed = lax.dynamic_slice_in_dim(tri_normed, quadrant_share * q_rows, q_rows, 0)
    closing = jax.nn.sigmoid(apply_linear(own_normed, trio_sigmoid_matrix)).reshape(
        q_rows, c_block, -1
    )
    change = apply_linear(product_normed, trio_final_matrix).reshape(q_rows, c_block, -1)
    out_rows = (mid_rows.astype(jnp.float32) + closing * change).astype(jnp.bfloat16)
    pairwise_output = lax.all_gather(out_rows, "branch", axis=0, tiled=True)
    return (revised_homolog_matrix, pairwise_output)


F32 = jnp.float32
BF16 = jnp.bfloat16
AXES = ("branch", "row", "col")
LANES = 128
HALF = LANES // 2
QUART = LANES // 4


def lane_of(shape):
    return lax.broadcasted_iota(jnp.int32, shape, len(shape) - 1)


def roll(x, shift):
    shift %= x.shape[-1]
    return pltpu.roll(x, shift, x.ndim - 1) if shift else x


def dot_nn(a, b):
    return jnp.dot(a, b, preferred_element_type=F32)


def dot_nt(a, b):
    return lax.dot_general(a, b, (((1,), (1,)), ((), ())), preferred_element_type=F32)


def call(body, outs, scratch=(), flops=10**6, mib=8, sems=0, anywhere=0, out_hbm=0, alias=None):
    scratch = [pltpu.VMEM(s, d) for s, d in scratch]
    scratch += [pltpu.SemaphoreType.DMA] * sems
    far, near = pl.BlockSpec(memory_space=pltpu.HBM), pl.BlockSpec(memory_space=pltpu.VMEM)

    def run(*args):
        specs = {}
        if anywhere:
            specs["in_specs"] = [far] * anywhere + [near] * (len(args) - anywhere)
        if out_hbm:
            specs["out_specs"] = (far,) * out_hbm
        args = [
            pltpu.with_memory_space_constraint(x, pltpu.HBM) if n < anywhere else x
            for n, x in enumerate(args)
        ]
        return pl.pallas_call(
            body,
            out_shape=tuple(jax.ShapeDtypeStruct(s, d) for s, d in outs),
            scratch_shapes=scratch,
            compiler_params=pltpu.CompilerParams(vmem_limit_bytes=mib * 2**20),
            cost_estimate=pl.CostEstimate(flops=flops, bytes_accessed=2**19, transcendentals=0),
            input_output_aliases=alias or {},
            **specs,
        )(*args)

    return run


def project_body(
    rows, hom_h, left_h, right_h, couple_h, outer_h, offset_h, first_h, second_h,
    normed, left_t, right_t, couple, outer_w, offset, gates_w, scr, hom, left_w, right_w, *sems,
):
    parts = 2
    cut = hom.shape[0] // parts
    pieces = [pl.ds(n * cut, cut) for n in range(parts)]
    pairs = [(hom_h.at[p], hom.at[p]) for p in pieces]
    pairs += [(left_h, left_w), (right_h, right_w), (couple_h, couple), (outer_h, outer_w)]
    pairs += [(offset_h, offset), (first_h, gates_w.at[pl.ds(0, 2)])]
    pairs += [(second_h, gates_w.at[pl.ds(2, 2)])]
    moves = [pltpu.make_async_copy(src, dst, sem) for (src, dst), sem in zip(pairs, sems)]
    for move in moves[: parts + 2]:
        move.start()
    n_rows, depth = hom.shape
    share = n_rows // rows
    width = left_w.shape[0]
    step = 2
    for first in range(0, share, step):
        if first * rows % cut == 0:
            moves[first * rows // cut].wait()
        if first == 0:
            for move in moves[parts + 2 :]:
                move.start()
        x = hom[first * rows : (first + step) * rows, :].astype(F32)
        x = x - jnp.mean(x, axis=-1, keepdims=True)
        x = x * lax.rsqrt(jnp.mean(x * x, axis=-1, keepdims=True) + EPS)
        normed[first * rows : (first + step) * rows, :] = x.astype(BF16)
        for s in range(step):
            piece = x[s * rows : (s + 1) * rows, :]
            for part in range(depth // LANES):
                scr[part, pl.ds(first + s, rows, stride=share), :] = piece[
                    :, part * LANES : (part + 1) * LANES
                ]
    moves[parts].wait()
    moves[parts + 1].wait()
    weights = jnp.concatenate([left_w[...], right_w[...]], axis=0)
    acc = 0
    for part in range(depth // LANES):
        acc = acc + dot_nt(
            weights[:, part * LANES : (part + 1) * LANES], scr[part].astype(BF16)
        )
    for g in range(n_rows // LANES):
        cut = slice(g * LANES, (g + 1) * LANES)
        left_t[g * width : (g + 1) * width, :] = acc[:width, cut].astype(BF16)
        right_t[g * width : (g + 1) * width, :] = acc[width:, cut].astype(BF16)
    for move in moves[parts + 2 :]:
        move.wait()


def heads_body(normed, key_w, value_w, query_w, gate_w, kv, query, gate):
    half = normed.shape[0] // 2
    x = normed[...]
    low = lane_of((half, LANES)) < HALF

    def both(w0, w1):
        y = dot_nt(x, jnp.concatenate([w0[...], w1[...]], axis=0))
        top, bottom = y[:half], y[half:]
        return (
            jnp.where(low, top, roll(bottom, HALF)),
            jnp.where(low, roll(top, HALF), bottom),
        )

    k, v = both(key_w, value_w)
    kv[:half, :] = k.astype(BF16)
    kv[half:, :] = v.astype(BF16)
    q, g = both(query_w, gate_w)
    query[...] = q.astype(BF16)
    gate[...] = jax.nn.sigmoid(g)


def pair_body(width, couple, offset_t, outer_w, left_t, couple_t, message, outer_wt, scr, wscr):
    tiles = couple.shape[0] // LANES
    for t in range(tiles):
        x = jnp.transpose(couple[t * LANES : (t + 1) * LANES, :].astype(F32))
        couple_t[t] = x.astype(BF16)
        x = x - jnp.mean(x, axis=0, keepdims=True)
        x = x * lax.rsqrt(jnp.mean(x * x, axis=0, keepdims=True) + EPS)
        scr[pl.ds(t, offset_t.shape[0], stride=tiles), :] = dot_nn(offset_t[...], x.astype(BF16))
    span = left_t.shape[0]
    message[:span, :] = left_t[...]
    message[span:, :] = scr[...].astype(BF16)
    wscr[...] = outer_w[...].astype(F32)
    per = LANES // width
    for g in range(width // per):
        block = jnp.concatenate(
            [wscr[pl.ds(g * per + q, width, stride=width), :] for q in range(per)], axis=0
        )
        outer_wt[:, g * LANES : (g + 1) * LANES] = jnp.transpose(block).astype(BF16)


def gate_tiles(scr, norm_t, w_own, w_far, first):
    tiles = norm_t.shape[0]
    weights = jnp.concatenate(
        [w_own[first], w_far[first], w_own[first + 1], w_far[first + 1]], axis=0
    )
    half = weights.shape[0] // 2
    for t in range(0, tiles, 2):
        y = dot_nn(weights, jnp.concatenate([norm_t[t], norm_t[t + 1]], axis=1))
        gated = jax.nn.sigmoid(y[half:]) * y[:half]
        store_gated(scr, t, 2 * tiles, gated[:, :LANES])
        store_gated(scr, t + 1, 2 * tiles, gated[:, LANES:])


def store_gated(scr, t, rows, gated):
    chans = gated.shape[0] // 2
    low = lane_of((chans, LANES)) < HALF
    a, b = gated[:chans], gated[chans:]
    scr[pl.ds(2 * t, chans, stride=rows), :] = jnp.where(low, a, roll(b, HALF))
    scr[pl.ds(2 * t + 1, chans, stride=rows), :] = jnp.where(low, roll(a, HALF), b)


def outer_body(
    total_rows, couple_t, outer_wt, left_own, left_far, own_r, sib_r, got, got_sib,
    mid_t, norm_t, lhs, rscr, mscr,
):
    col = lax.axis_index("col")
    row = lax.axis_index("row")
    chip_y, core = row // 2, row % 2
    width = lhs.shape[0] // couple_t.shape[0]
    span = own_r.shape[0] // width * LANES
    tiles = couple_t.shape[0]
    rows = 2 * tiles
    share = span // rows
    block = rows * 2
    group = lane_of((width, LANES)) // share
    own_first = col == 0
    for g in range(span // LANES):
        cut = slice(g * width, (g + 1) * width)
        own, far = left_own[cut, :].astype(F32), left_far[cut, :].astype(F32)
        a, b = jnp.where(own_first, own, far), jnp.where(own_first, far, own)
        even = jnp.where(
            group == 0, a,
            jnp.where(group == 1, roll(b, QUART), jnp.where(group == 2, roll(a, QUART), roll(b, HALF))),
        )
        odd = jnp.where(
            group == 0, roll(a, HALF),
            jnp.where(group == 1, roll(b, -QUART), jnp.where(group == 2, roll(a, -QUART), b)),
        )
        lhs[2 * g * width : (2 * g + 1) * width, :] = even.astype(BF16)
        lhs[(2 * g + 1) * width : (2 * g + 2) * width, :] = odd.astype(BF16)
    here, north = chip_y == col, core == 0
    size = own_r.shape[0]
    for a in range(2):
        for g in range(span // LANES):
            cut = slice(g * width, (g + 1) * width)
            same = slice(a * size + g * width, a * size + (g + 1) * width)
            flip = slice((1 - a) * size + g * width, (1 - a) * size + (g + 1) * width)
            from_0 = jnp.where(north, got[same, :], got_sib[same, :])
            from_1 = jnp.where(north, got_sib[flip, :], got[flip, :])
            local = jnp.where(core == a, own_r[cut, :], sib_r[cut, :])
            one = jnp.where(here, local, from_0).astype(F32)
            two = jnp.where(here, from_0, from_1).astype(F32)
            t0, t1 = jnp.where(own_first, one, two), jnp.where(own_first, two, one)
            for j4 in range(LANES // share):
                j = a * rows + g * (LANES // share) + j4
                tile = jnp.where(
                    group == 0, roll(t0, -share * j4),
                    jnp.where(group == 1, roll(t1, share - share * j4), 0.0),
                )
                rscr[pl.ds(j, width, stride=2 * block), :] = tile
                rscr[pl.ds(block + j, width, stride=2 * block), :] = roll(tile, HALF)
    left = lhs[...]
    for q in range(0, width, 2):
        rhs = rscr[q * LANES : (q + 2) * LANES, :].astype(BF16)
        prod = dot_nt(left, rhs).astype(BF16)
        for t in range(tiles):
            for e in range(2):
                mscr[t, (q + e) * width : (q + e + 1) * width, :] = prod[
                    t * width : (t + 1) * width, e * LANES : (e + 1) * LANES
                ]
    for t in range(0, tiles, 2):
        both = dot_nn(outer_wt[...], jnp.concatenate([mscr[t], mscr[t + 1]], axis=1))
        for e in range(2):
            update = both[:, e * LANES : (e + 1) * LANES] * (1.0 / total_rows)
            mid = (couple_t[t + e].astype(F32) + update).astype(BF16)
            mid_t[t + e] = mid
            x = mid.astype(F32)
            x = x - jnp.mean(x, axis=0, keepdims=True)
            x = x * lax.rsqrt(jnp.mean(x * x, axis=0, keepdims=True) + EPS)
            norm_t[t + e] = x.astype(BF16)


def right_body(norm_t, w_own, w_far, right_pk, gscr):
    gate_tiles(gscr, norm_t, w_own, w_far, 2)
    right_pk[...] = gscr[...].astype(BF16)


def left_body(norm_t, w_own, w_far, left_pk, gscr):
    gate_tiles(gscr, norm_t, w_own, w_far, 0)
    left_pk[...] = gscr[...].astype(BF16)


def close_body(norm_t, close_w, close_t):
    w_close = jnp.transpose(close_w[...].astype(F32)).astype(BF16)
    for t in range(norm_t.shape[0]):
        close_t[t] = jax.nn.sigmoid(dot_nn(w_close, norm_t[t]))


def triangle_body(rows, part, left_pk, own, sib, across, across_sib, mine, other):
    col = lax.axis_index("col")
    row = lax.axis_index("row")
    chip_y, core = row // 2, row % 2
    is_low, here = core == 0, chip_y == col
    n = rows // 2
    low = lane_of((n, LANES)) < HALF
    for ch in range(left_pk.shape[0] // rows):
        cut = slice(ch * rows, (ch + 1) * rows)
        a = left_pk[ch * rows + part * n : ch * rows + (part + 1) * n, :]
        zero = jnp.zeros_like(a)
        lhs = jnp.concatenate([jnp.where(low, a, zero), jnp.where(low, zero, a)], axis=0)
        o, s, x, xs = own[cut, :], sib[cut, :], across[cut, :], across_sib[cut, :]
        n0, n1 = jnp.where(is_low, o, s), jnp.where(is_low, s, o)
        f0, f1 = jnp.where(is_low, x, xs), jnp.where(is_low, xs, x)
        rhs = jnp.concatenate(
            [
                jnp.where(here, n0, f0), jnp.where(here, n1, f1),
                jnp.where(here, f0, n0), jnp.where(here, f1, n1),
            ],
            axis=0,
        )
        prod = dot_nt(lhs, rhs)
        u, v = prod[:n], prod[n:]
        to = slice(ch * n, (ch + 1) * n)
        mine[to, :] = jnp.where(low, u, roll(v, HALF))
        other[to, :] = jnp.where(low, roll(u, HALF), v).astype(BF16)


def final_body(n, part, *refs):
    half_own, half_far, mid_t, close_t, final_w, out_h, scr, out, *sems = refs[part:]
    branch = lax.axis_index("branch")
    chans = half_own.shape[0] // n
    low = lane_of((chans, LANES)) < HALF
    scr[0] = half_own[...].astype(F32)
    scr[1] = half_far[...].astype(F32)
    owners = [branch, branch ^ 2, branch ^ 1, branch ^ 3]
    w_t = [final_w[pl.ds(pl.multiple_of(o * chans, chans), chans), :] for o in owners]
    w_t = jnp.transpose(jnp.concatenate(w_t, axis=0).astype(F32)).astype(BF16)
    tiles = n // 2
    per = tiles // len(sems)
    base = part * tiles
    moves = []
    for t in range(tiles):
        blocks = []
        for h in range(2):
            z0 = scr[h, pl.ds(2 * t, chans, stride=n), :]
            z1 = scr[h, pl.ds(2 * t + 1, chans, stride=n), :]
            blocks += [jnp.where(low, z0, roll(z1, HALF)), jnp.where(low, roll(z0, HALF), z1)]
        x = jnp.concatenate(blocks, axis=0)
        x = x - jnp.mean(x, axis=0, keepdims=True)
        x = x * lax.rsqrt(jnp.mean(x * x, axis=0, keepdims=True) + EPS)
        change = dot_nn(w_t, x.astype(BF16))
        result = mid_t[base + t].astype(F32) + close_t[base + t] * change
        out[t * LANES : (t + 1) * LANES, :] = jnp.transpose(result).astype(BF16)
        if t % per == per - 1:
            here = out.at[pl.ds((t + 1 - per) * LANES, per * LANES)]
            there = out_h.at[pl.ds((base + t + 1 - per) * LANES, per * LANES)]
            moves.append(pltpu.make_async_copy(here, there, sems[t // per]))
            moves[-1].start()
    for move in moves:
        move.wait()


def attend_body(
    rows, head, query, gate, own, sib, across, across_sib, sent, got, w_out, *rest
):
    outs, (bscr, cscr) = rest[:-2], rest[-2:]
    col = lax.axis_index("col")
    row = lax.axis_index("row")
    branch = lax.axis_index("branch")
    top, is_low = row // 2 == 0, row % 2 == 0
    half = query.shape[0]
    scale = float(head) ** (-0.5)
    n_bias = bscr.shape[0] // 2
    start = sent.shape[0] - n_bias
    b_own, b_far = sent[start:, :].astype(F32), got[start:, :].astype(F32)
    b0, b1 = jnp.where(col == 0, b_own, b_far), jnp.where(col == 0, b_far, b_own)
    low = lane_of((n_bias, LANES)) < HALF
    bscr[pl.ds(0, n_bias, stride=2), :] = jnp.where(low, b0, roll(b1, HALF))
    bscr[pl.ds(1, n_bias, stride=2), :] = jnp.where(low, roll(b0, HALF), b1)
    bias = jnp.transpose(jnp.concatenate([bscr[...], bscr[...]], axis=0))
    b = [bias[n * rows : (n + 1) * rows] for n in range(LANES // rows)]
    b = [jnp.where(is_low, b[n], b[n ^ 1]) for n in range(len(b))]
    b = [jnp.where(top, b[n], b[n ^ 2]) for n in range(len(b))]
    bias = jnp.concatenate(b, axis=0)
    group = lane_of((rows, LANES)) // head

    def gather(at):
        cut = pl.ds(pl.multiple_of(at, rows), rows)
        return jnp.concatenate([own[cut, :], sib[cut, :], across[cut, :], across_sib[cut, :]], axis=0)

    batch = 4

    def some(step, carry):
        spots = [(step * batch + n) * rows for n in range(batch)]
        cuts = [pl.ds(pl.multiple_of(at, rows), rows) for at in spots]
        masked = []
        for cut in cuts:
            q = query[cut, :]
            zero = jnp.zeros_like(q)
            masked.append(
                jnp.concatenate(
                    [jnp.where(group == g, q, zero) for g in range(LANES // head)], axis=0
                )
            )
        scores = [dot_nt(gather(at), q) * scale + bias for at, q in zip(spots, masked)]
        tops = [jnp.max(x, axis=0, keepdims=True) for x in scores]
        expo = [jnp.exp(x - top) for x, top in zip(scores, tops)]
        expo = [x * (1.0 / jnp.sum(x, axis=0, keepdims=True)) for x in expo]
        full = [
            lax.dot_general(
                x.astype(BF16), gather(half + at), (((0,), (0,)), ((), ())),
                preferred_element_type=F32,
            )
            for x, at in zip(expo, spots)
        ]
        for cut, x in zip(cuts, full):
            ctx = x[:rows]
            for g in range(1, LANES // head):
                ctx = jnp.where(group == g, x[g * rows : (g + 1) * rows], ctx)
            cscr[cut, :] = (ctx * gate[cut, :]).astype(BF16)
        return carry

    lax.fori_loop(0, half // rows // batch, some, 0, unroll=True)
    ctx = cscr[...]
    low = lane_of((w_out.shape[0], LANES)) < HALF
    for m in range(len(outs)):
        chunk = branch ^ m
        at = pl.multiple_of((chunk // 2) * LANES, LANES)
        w = w_out[:, pl.ds(at, LANES)].astype(F32)
        w = jnp.where(chunk % 2 == 0, w, roll(w, HALF))
        w = jnp.concatenate([jnp.where(low, w, 0.0), jnp.where(low, 0.0, roll(w, HALF))], axis=0)
        outs[m][...] = dot_nn(ctx, w.astype(BF16)).astype(BF16)


def revise_body(hom, p0, p1, p2, p3, out):
    branch = lax.axis_index("branch")
    acc = p0[...].astype(F32) + p1[...].astype(F32)
    acc = acc + p2[...].astype(F32) + p3[...].astype(F32)
    n = acc.shape[0]
    at = pl.multiple_of((branch // 2) * LANES, LANES)
    base = hom[:, pl.ds(at, LANES)].astype(F32)
    base = jnp.where(branch % 2 == 0, base, roll(base, HALF))
    out[:n, :] = (acc + base[:n])[:, :HALF].astype(BF16)
    out[n:, :] = (roll(acc, HALF) + base[n:])[:, :HALF].astype(BF16)


def fast_per_device(
    mesh,
    homolog_tensor,
    couple_tensor,
    probe_matrix,
    lookup_matrix,
    content_matrix,
    scoring_sigmoid_matrix,
    scoring_final_matrix,
    couple_offset_matrix,
    product_first_matrix,
    product_second_matrix,
    product_final_matrix,
    trio_first_matrix,
    trio_second_matrix,
    trio_sigmoid_matrix,
    trio_final_matrix,
):
    n_b, n_r, n_c = (mesh.shape[a] for a in AXES)

    def send(x, source):
        pairs = []
        for b in range(n_b):
            for r in range(n_r):
                for c in range(n_c):
                    if (origin := source(b, r, c)) is not None:
                        sb, sr, sc = origin
                        pairs.append(((sb * n_r + sr) * n_c + sc, (b * n_r + r) * n_c + c))
        return lax.ppermute(x, AXES, pairs)

    def other_col(b, r, c):
        return b, r, c ^ 1

    def other_core(b, r, c):
        return b, r ^ 1, c

    def other_chip(b, r, c):
        return b, r ^ 2, c

    def turned(b, r, c):
        y, core = r // 2, r % 2
        if y == c:
            return None if core else (b, r, c ^ 1)
        return b, 2 * c + core, c ^ core

    share, rows, depth = homolog_tensor.shape
    block = couple_tensor.shape[1]
    chans = couple_tensor.shape[2]
    width = product_first_matrix.shape[1]
    heads_w = probe_matrix.shape[1]
    local_heads = couple_offset_matrix.shape[1]
    head = heads_w // local_heads
    quarter = trio_first_matrix.shape[2]
    tiles = rows * block // LANES
    n_rows = share * rows
    hom = homolog_tensor.reshape(n_rows, depth)
    couple = couple_tensor.reshape(rows * block, chans)

    flat = (n_rows * width // LANES, LANES)
    normed, left_t, right_t, couple_v, outer_w, offset_t, w_own = call(
        functools.partial(project_body, rows),
        [
            ((n_rows, depth), BF16), (flat, BF16), (flat, BF16),
            (couple.shape, BF16), (product_final_matrix.shape, BF16),
            ((local_heads, chans), BF16), ((4, quarter, chans), BF16),
        ],
        [
            ((depth // LANES, n_rows, LANES), F32), ((n_rows, depth), BF16),
            ((width, depth), BF16), ((width, depth), BF16),
        ],
        sems=9,
        anywhere=8,
    )(
        hom, product_first_matrix.T, product_second_matrix.T, couple, product_final_matrix,
        couple_offset_matrix.T, jnp.transpose(trio_first_matrix, (0, 2, 1)),
        jnp.transpose(trio_second_matrix, (0, 2, 1)),
    )
    sib_r = send(right_t, other_core)
    got_r = send(jnp.concatenate([right_t, sib_r], axis=0), turned)
    couple_t, message, outer_wt = call(
        functools.partial(pair_body, width),
        [
            ((tiles, chans, LANES), BF16),
            ((flat[0] + local_heads * tiles, LANES), BF16),
            ((chans, width * width), BF16),
        ],
        [((local_heads * tiles, LANES), F32), ((width * width, chans), F32)],
    )(couple_v, offset_t, outer_w, left_t)
    got = send(message, other_col)
    kv, query, gate = call(
        heads_body,
        [((n_rows, LANES), BF16), ((n_rows // 2, LANES), BF16), ((n_rows // 2, LANES), F32)],
    )(normed, lookup_matrix.T, content_matrix.T, probe_matrix.T, scoring_sigmoid_matrix.T)
    kv_x = send(kv, other_chip)
    kv_s = send(kv, other_core)
    kv_xs = send(kv_x, other_core)
    w_far = send(w_own, lambda b, r, c: (b ^ 2, r, c))
    got_rs = send(got_r, other_core)

    mid_t, norm_t = call(
        functools.partial(outer_body, share * n_c),
        [((tiles, chans, LANES), BF16), ((tiles, chans, LANES), BF16)],
        [
            ((tiles * width, LANES), BF16),
            ((width * LANES, LANES), F32),
            ((tiles, width * width, LANES), BF16),
        ],
        mib=16,
    )(couple_t, outer_wt, message, got, right_t, sib_r, got_r, got_rs)
    (right_pk,) = call(
        right_body, [((quarter * rows, LANES), BF16)], [((quarter * rows, LANES), F32)]
    )(norm_t, w_own, w_far)
    right_x = send(right_pk, other_chip)
    right_s = send(right_pk, other_core)
    (left_pk,) = call(
        left_body, [((quarter * rows, LANES), BF16)], [((quarter * rows, LANES), F32)]
    )(norm_t, w_own, w_far)
    parts = call(
        functools.partial(attend_body, rows, head),
        [((n_rows // 2, LANES), BF16)] * n_b,
        [((local_heads * rows, LANES), F32), ((n_rows // 2, LANES), BF16)],
    )(query, gate, kv, kv_s, kv_x, kv_xs, message, got, scoring_final_matrix)
    right_xs = send(right_x, other_core)

    mines, fars = [], []
    for part in range(2):
        mine, other = call(
            functools.partial(triangle_body, rows, part),
            [((quarter * rows // 2, LANES), F32), ((quarter * rows // 2, LANES), BF16)],
        )(left_pk, right_pk, right_s, right_x, right_xs)
        mines.append(mine)
        fars.append(send(other, other_col))
    (close_t,) = call(close_body, [((tiles, chans, LANES), F32)])(norm_t, trio_sigmoid_matrix)
    parts = [parts[0]] + [send(parts[m], lambda b, r, c, m=m: (b ^ m, r, c)) for m in range(1, n_b)]
    half_own = [(mine + far.astype(F32)).astype(BF16) for mine, far in zip(mines, fars)]
    half_far = [send(half, lambda b, r, c: (b ^ 1, r, c)) for half in half_own]
    (revised,) = call(revise_body, [((n_rows, depth // n_b), BF16)])(hom, *parts)

    pair_out = ()
    for part in range(2):
        pair_out = call(
            functools.partial(final_body, rows // 2, part),
            [((rows * block, chans), BF16)],
            [((2, quarter * rows // 2, LANES), F32), ((rows * block // 2, chans), BF16)],
            mib=12,
            sems=2,
            out_hbm=1,
            anywhere=part,
            alias={0: 0} if part else None,
        )(*pair_out, half_own[part], half_far[part], mid_t, close_t, trio_final_matrix)
    (pair_out,) = pair_out
    return (
        revised.reshape(share, rows, depth // n_b),
        pair_out.reshape(rows, block, chans),
    )


def fits(mesh, args):
    hom, couple = args[0], args[1]
    share, rows, depth = hom.shape
    return (
        mesh.shape["branch"] == 4
        and mesh.shape["row"] == 4
        and mesh.shape["col"] == 2
        and couple.shape[0] == rows
        and couple.shape[1] == 2 * rows == HALF
        and couple.shape[2] == LANES
        and share == QUART
        and args[2].shape[1] == HALF
        and depth == 4 * HALF
        and args[8].shape[1] == QUART
        and args[11].shape[2] == QUART
        and args[7].shape[1] == 2
    )


def dispatch(mesh, *args):
    if fits(mesh, args):
        return fast_per_device(mesh, *args)
    return plain_per_device(*args)


def solution(mesh):
    return jax.shard_map(
        functools.partial(dispatch, mesh),
        mesh=mesh,
        in_specs=(
            P("col", "row", None),
            P("row", "col", None),
            P(None, "branch"),
            P(None, "branch"),
            P(None, "branch"),
            P(None, "branch"),
            P("branch", None),
            P(None, "branch"),
            P(),
            P(),
            P(),
            P(None, None, "branch"),
            P(None, None, "branch"),
            P(),
            P(),
        ),
        out_specs=(P("col", "row", "branch"), P("row", "col", None)),
        check_vma=False,
    )
```

profile of v0, /device:TPU:0, one launch (start us, length us, event | category | flops | bytes accessed | tf_op | source)
XLA Modules:
  0.0 60.7 jit_solution(4408292238398607360)
XLA Ops:
  0.6 2.8 %shard_map.158 = (bf16[1024,256]{1,0:T(8,128)(2,1)S(1)}, bf16[256,128]{1,0:T(8,128)(2,1)S(1)}, bf16[256,128]{1,0:T(8,128)(2,1)S(1)}, bf16[2048,128]{1,0:T(8,128)...) custom-call(bf16[1024,256]{1,0:T(8,128)(2,1)} %bitcast.13, ...), custom_call_target="tpu_custom_call" | custom-call | flops 1000000 | bytes 524288 | tf_op jit(solution)/shard_map/pallas_call | solution.py:216
  3.4 0.6 collective-permute-start.7
  4.0 0.9 %collective-permute-done.7.sib_r = bf16[256,128]{1,0:T(8,128)(2,1)S(1)} collective-permute-done((bf16[256,128]{1,0:T(8,128)(2,1)S(1)}, bf16[256,128]{1,0:T(8,128)(2,1)S(1)}, u32[]{:S(2)}, u32[]{:S(2)}) %collective-permute-start.7) | collective-permute-done | bytes 65568 | tf_op jit(solution)/shard_map/ppermute | solution.py:604
  4.9 4.8 %collective-permute-start.8 = (bf16[512,128]{1,0:T(8,128)(2,1)S(1)}, bf16[512,128]{1,0:T(8,128)(2,1)S(1)}, u32[]{:S(2)}, u32[]{:S(2)}) collective-permute-start(bf16[512,128]{1,0:T(8,128)(2,1)S(1)} %pad_maximum_fusion), channel_id=1, source_target_pairs={{1,0},{5,1},{6,3},{0,4},{4,5},{3,6},{9,8},{13,9},{14,11},{8,12},{1... | collective-permute-start | bytes 393224 | tf_op jit(solution)/shard_map/ppermute | solution.py:604
  9.7 3.9 %collective-permute-done.8.got = bf16[512,128]{1,0:T(8,128)(2,1)S(1)} collective-permute-done((bf16[512,128]{1,0:T(8,128)(2,1)S(1)}, bf16[512,128]{1,0:T(8,128)(2,1)S(1)}, u32[]{:S(2)}, u32[]{:S(2)}) %collective-permute-start.8) | collective-permute-done | bytes 131104 | tf_op jit(solution)/shard_map/ppermute | solution.py:604
  13.6 0.0 collective-permute-start.9
  13.6 0.8 %shard_map.160 = (bf16[16,128,128]{2,1,0:T(8,128)(2,1)S(1)}, bf16[288,128]{1,0:T(8,128)(2,1)S(1)}, bf16[128,1024]{1,0:T(8,128)(2,1)S(1)}) custom-call(bf16[2048,128]{1,0:T(8,128)(2,1)S(1)} %get-tuple-element.29.couple, bf16[2,128]{1,0:T(2,128)(2,1)S(1)} %get-tuple-element.30.offset_t, bf16[1024,128]{1,0:T(8,128)(2,1)S(1)} %get-tuple-element.31.outer_w, ...), custom_call_target="tpu_custom_call" | custom-call | flops 1000000 | bytes 524288 | tf_op jit(solution)/shard_map/pallas_call | solution.py:216
  14.4 2.5 %collective-permute-start.3 = (bf16[288,128]{1,0:T(8,128)(2,1)S(1)}, bf16[288,128]{1,0:T(8,128)(2,1)S(1)}, u32[]{:S(2)}, u32[]{:S(2)}) collective-permute-start(bf16[288,128]{1,0:T(8,128)(2,1)S(1)} %get-tuple-element.33.sent.left_own), channel_id=1, source_target_pairs={{1,0},{0,1},{3,2},{2,3},{5,4},{4,5},{7,6},{6,7},{9,8},{8,9},{11,10... | collective-permute-start | bytes 221192 | tf_op jit(solution)/shard_map/ppermute | solution.py:604
  16.8 2.6 %collective-permute-start.10 = (bf16[4,32,128]{2,1,0:T(8,128)(2,1)S(1)}, bf16[4,32,128]{2,1,0:T(8,128)(2,1)S(1)}, u32[]{:S(2)}, u32[]{:S(2)}) collective-permute-start(bf16[4,32,128]{2,1,0:T(8,128)(2,1)S(1)} %get-tuple-element.42.w_own), channel_id=1, source_target_pairs={{16,0},{17,1},{18,2},{19,3},{20,4},{21,5},{22,6},{23,7},{24,8},{25... | collective-permute-start | bytes 98312 | tf_op jit(solution)/shard_map/ppermute | solution.py:604
  19.4 0.4 collective-permute-done.3.got.left_far
  19.8 0.0 collective-permute-done.9.got_sib
  19.8 3.2 %shard_map.163 = (bf16[16,128,128]{2,1,0:T(8,128)(2,1)S(1)}, bf16[16,128,128]{2,1,0:T(8,128)(2,1)S(1)}) custom-call(bf16[16,128,128]{2,1,0:T(8,128)(2,1)S(1)} %get-tuple-element.38.couple_t, bf16[128,1024]{1,0:T(8,128)(2,1)S(1)} %get-tuple-element.39.outer_wt, bf16[288,128]{1,0:T(8,128)(2,1)S(1)} %get-tuple-element.33.sent.left_own, ...), custom_call_target="tpu_custom_call" | custom-call | flops 1000000 | bytes 524288 | tf_op jit(solution)/shard_map/pallas_call | solution.py:216
  23.0 0.0 collective-permute-done.10.w_far
  23.0 0.0 copy-start.2
  23.0 0.0 copy-start.3
  23.0 0.0 copy-start.4
  23.1 0.0 copy-start.5
  23.1 0.7 %shard_map.165.own = bf16[1024,128]{1,0:T(8,128)(2,1)S(1)} custom-call(bf16[16,128,128]{2,1,0:T(8,128)(2,1)S(1)} %get-tuple-element.41.norm_t, bf16[4,32,128]{2,1,0:T(8,128)(2,1)S(1)} %get-tuple-element.42.w_own, bf16[4,32,128]{2,1,0:T(8,128)(2,1)S(1)} %collective-permute-done.10.w_far), custom_call_target="tpu_custom_call" | custom-call | flops 1000000 | bytes 524288 | tf_op jit(solution)/shard_map/pallas_call | solution.py:216
  23.8 1.8 %collective-permute-start.12 = (bf16[1024,128]{1,0:T(8,128)(2,1)S(1)}, bf16[1024,128]{1,0:T(8,128)(2,1)S(1)}, u32[]{:S(2)}, u32[]{:S(2)}) collective-permute-start(bf16[1024,128]{1,0:T(8,128)(2,1)S(1)} %shard_map.165.own), channel_id=1, source_target_pairs={{4,0},{5,1},{6,2},{7,3},{0,4},{1,5},{2,6},{3,7},{12,8},{13,9},{14,... | collective-permute-start | bytes 786440 | tf_op jit(solution)/shard_map/ppermute | solution.py:604
  25.6 0.0 copy-done.2
  25.6 0.0 copy-done.3
  25.6 0.0 copy-done.4
  25.6 0.0 copy-done.5
  25.6 0.5 shard_map.159
  26.1 0.3 collective-permute-start.1
  26.5 0.0 collective-permute-start.11
  26.5 6.6 %collective-permute-done.12.across = bf16[1024,128]{1,0:T(8,128)(2,1)S(1)} collective-permute-done((bf16[1024,128]{1,0:T(8,128)(2,1)S(1)}, bf16[1024,128]{1,0:T(8,128)(2,1)S(1)}, u32[]{:S(2)}, u32[]{:S(2)}) %collective-permute-start.12) | collective-permute-done | bytes 262176 | tf_op jit(solution)/shard_map/ppermute | solution.py:604
  33.0 0.0 collective-permute-start.13
  33.0 0.5 collective-permute-start
  33.5 4.1 %collective-permute-done.1.across = bf16[1024,128]{1,0:T(8,128)(2,1)S(1)} collective-permute-done((bf16[1024,128]{1,0:T(8,128)(2,1)S(1)}, bf16[1024,128]{1,0:T(8,128)(2,1)S(1)}, u32[]{:S(2)}, u32[]{:S(2)}) %collective-permute-start.1) | collective-permute-done | bytes 262176 | tf_op jit(solution)/shard_map/ppermute | solution.py:604
  37.6 0.0 collective-permute-start.2
  37.6 0.7 %shard_map.164.left_pk = bf16[1024,128]{1,0:T(8,128)(2,1)S(1)} custom-call(bf16[16,128,128]{2,1,0:T(8,128)(2,1)S(1)} %get-tuple-element.41.norm_t, bf16[4,32,128]{2,1,0:T(8,128)(2,1)S(1)} %get-tuple-element.42.w_own, bf16[4,32,128]{2,1,0:T(8,128)(2,1)S(1)} %collective-permute-done.10.w_far), custom_call_target="tpu_custom_call" | custom-call | flops 1000000 | bytes 524288 | tf_op jit(solution)/shard_map/pallas_call | solution.py:216
  38.3 0.0 copy-start.6
  38.3 0.0 collective-permute-done.11.sib
  38.4 0.0 collective-permute-done.13.across_sib
  38.4 0.8 %shard_map.166 = (f32[512,128]{1,0:T(8,128)S(1)}, bf16[512,128]{1,0:T(8,128)(2,1)S(1)}) custom-call(bf16[1024,128]{1,0:T(8,128)(2,1)S(1)} %shard_map.164.left_pk, bf16[1024,128]{1,0:T(8,128)(2,1)S(1)} %shard_map.165.own, bf16[1024,128]{1,0:T(8,128)(2,1)S(1)} %collective-permute-done.11.sib, bf16[1024,128]{1,0:T(8,128)(2,1)S(1)} %collective-permute-done.12.across, ...), custom_call_target="tpu_custom_call" | custom-call | flops 1000000 | bytes 524288 | tf_op jit(solution)/shard_map/pallas_call | solution.py:216
  39.1 1.5 %collective-permute-start.14 = (bf16[512,128]{1,0:T(8,128)(2,1)S(1)}, bf16[512,128]{1,0:T(8,128)(2,1)S(1)}, u32[]{:S(2)}, u32[]{:S(2)}) collective-permute-start(bf16[512,128]{1,0:T(8,128)(2,1)S(1)} %get-tuple-element.44), channel_id=1, source_target_pairs={{1,0},{0,1},{3,2},{2,3},{5,4},{4,5},{7,6},{6,7},{9,8},{8,9},{11,10... | collective-permute-start | bytes 393224 | tf_op jit(solution)/shard_map/ppermute | solution.py:604
  40.6 0.0 collective-permute-done.sib
  40.6 0.0 collective-permute-done.2.across_sib
  40.6 0.0 copy-done.6
  40.7 1.7 %shard_map.161 = (bf16[512,128]{1,0:T(8,128)(2,1)S(1)}, bf16[512,128]{1,0:T(8,128)(2,1)S(1)}, bf16[512,128]{1,0:T(8,128)(2,1)S(1)}, bf16[512,128]{1,0:T(8,128)(2,1)S(1)}) custom-call(bf16[512,128]{1,0:T(8,128)(2,1)S(1)} %get-tuple-element.26.query, f32[512,128]{1,0:T(8,128)S(1)} %get-tuple-element.27.gate, bf16[1024,128]{1,0:T(8,128)(2,1)S(1)} %get-tuple-element.28.own, ...), custom_call_target="tpu_custom_call" | custom-call | flops 1000000 | bytes 524288 | tf_op jit(solution)/shard_map/pallas_call | solution.py:216
  42.4 1.6 %collective-permute-start.4 = (bf16[512,128]{1,0:T(8,128)(2,1)S(1)}, bf16[512,128]{1,0:T(8,128)(2,1)S(1)}, u32[]{:S(2)}, u32[]{:S(2)}) collective-permute-start(bf16[512,128]{1,0:T(8,128)(2,1)S(1)} %get-tuple-element.35), channel_id=1, source_target_pairs={{8,0},{9,1},{10,2},{11,3},{12,4},{13,5},{14,6},{15,7},{0,8},{1,9},... | collective-permute-start | bytes 393224 | tf_op jit(solution)/shard_map/ppermute | solution.py:604
  44.0 2.6 %collective-permute-start.5 = (bf16[512,128]{1,0:T(8,128)(2,1)S(1)}, bf16[512,128]{1,0:T(8,128)(2,1)S(1)}, u32[]{:S(2)}, u32[]{:S(2)}) collective-permute-start(bf16[512,128]{1,0:T(8,128)(2,1)S(1)} %get-tuple-element.36), channel_id=1, source_target_pairs={{16,0},{17,1},{18,2},{19,3},{20,4},{21,5},{22,6},{23,7},{24,8},{25... | collective-permute-start | bytes 393224 | tf_op jit(solution)/shard_map/ppermute | solution.py:604
  46.6 0.2 collective-permute-start.6
  46.8 0.7 %shard_map.169 = (f32[512,128]{1,0:T(8,128)S(1)}, bf16[512,128]{1,0:T(8,128)(2,1)S(1)}) custom-call(bf16[1024,128]{1,0:T(8,128)(2,1)S(1)} %shard_map.164.left_pk, bf16[1024,128]{1,0:T(8,128)(2,1)S(1)} %shard_map.165.own, bf16[1024,128]{1,0:T(8,128)(2,1)S(1)} %collective-permute-done.11.sib, bf16[1024,128]{1,0:T(8,128)(2,1)S(1)} %collective-permute-done.12.across, ...), custom_call_target="tpu_custom_call" | custom-call | flops 1000000 | bytes 524288 | tf_op jit(solution)/shard_map/pallas_call | solution.py:216
  47.6 0.6 %collective-permute-start.16 = (bf16[512,128]{1,0:T(8,128)(2,1)S(1)}, bf16[512,128]{1,0:T(8,128)(2,1)S(1)}, u32[]{:S(2)}, u32[]{:S(2)}) collective-permute-start(bf16[512,128]{1,0:T(8,128)(2,1)S(1)} %get-tuple-element.47), channel_id=1, source_target_pairs={{1,0},{0,1},{3,2},{2,3},{5,4},{4,5},{7,6},{6,7},{9,8},{8,9},{11,10... | collective-permute-start | bytes 393224 | tf_op jit(solution)/shard_map/ppermute | solution.py:604
  48.2 0.0 collective-permute-done.14
  48.2 0.6 collective-permute-start.15
  48.8 3.8 %collective-permute-done.16 = bf16[512,128]{1,0:T(8,128)(2,1)S(1)} collective-permute-done((bf16[512,128]{1,0:T(8,128)(2,1)S(1)}, bf16[512,128]{1,0:T(8,128)(2,1)S(1)}, u32[]{:S(2)}, u32[]{:S(2)}) %collective-permute-start.16) | collective-permute-done | bytes 131104 | tf_op jit(solution)/shard_map/ppermute | solution.py:604
  52.6 0.0 copy-start.7
  52.6 0.0 copy-start
  52.7 0.7 %collective-permute-start.17 = (bf16[512,128]{1,0:T(8,128)(2,1)S(1)}, bf16[512,128]{1,0:T(8,128)(2,1)S(1)}, u32[]{:S(2)}, u32[]{:S(2)}) collective-permute-start(bf16[512,128]{1,0:T(8,128)(2,1)S(1)} %add_convert_fusion.refs_1_), channel_id=1, source_target_pairs={{8,0},{9,1},{10,2},{11,3},{12,4},{13,5},{14,6},{15,7},{0,8},{1,9},... | collective-permute-start | bytes 393224 | tf_op jit(solution)/shard_map/ppermute | solution.py:604
  53.4 0.0 copy-done.7
  53.4 0.4 shard_map.167.refs_3_.refs_4_
  53.8 0.0 collective-permute-done.4.p1
  53.8 3.2 %collective-permute-done.5.p2 = bf16[512,128]{1,0:T(8,128)(2,1)S(1)} collective-permute-done((bf16[512,128]{1,0:T(8,128)(2,1)S(1)}, bf16[512,128]{1,0:T(8,128)(2,1)S(1)}, u32[]{:S(2)}, u32[]{:S(2)}) %collective-permute-start.5) | collective-permute-done | bytes 131104 | tf_op jit(solution)/shard_map/ppermute | solution.py:604
  56.9 0.0 collective-permute-done.6.p3
  56.9 0.0 copy-done
  57.0 0.9 %shard_map.162 = bf16[1024,64]{1,0:T(8,128)(2,1)} custom-call(bf16[1024,256]{1,0:T(8,128)(2,1)S(1)} %bitcast.14, bf16[512,128]{1,0:T(8,128)(2,1)S(1)} %get-tuple-element.34.p0, bf16[512,128]{1,0:T(8,128)(2,1)S(1)} %collective-permute-done.4.p1, bf16[512,128]{1,0:T(8,128)(2,1)S(1)} %collective-permute-done.5.p2, bf16[512,128]{1,0:T(8,128)(2,1)S(1)} %collective-permute-done.6.p3), custom_call_target="tpu_custom_call" | custom-call | flops 1000000 | bytes 524288 | tf_op jit(solution)/shard_map/pallas_call | solution.py:216
  57.9 0.0 collective-permute-done.15.refs_1_
  57.9 0.0 copy-done.1
  57.9 1.3 %shard_map.168.refs_0_ = bf16[2048,128]{1,0:T(8,128)(2,1)} custom-call(bf16[512,128]{1,0:T(8,128)(2,1)S(1)} %add_convert_fusion.1.refs_0_, bf16[512,128]{1,0:T(8,128)(2,1)S(1)} %collective-permute-done.15.refs_1_, bf16[16,128,128]{2,1,0:T(8,128)(2,1)S(1)} %get-tuple-element.45.refs_2_.refs_3_, f32[16,128,128]{2,1,0:T(8,128)S(1)} %shard_map.167.refs_3_.refs_4_, ...), custom_call_target="tpu_custom_call" | custom-call | flops 1000000 | bytes 524288 | tf_op jit(solution)/shard_map/pallas_call | solution.py:216
  59.2 0.3 collective-permute-done.17.refs_2_
  59.4 1.3 %shard_map.170 = bf16[2048,128]{1,0:T(8,128)(2,1)} custom-call(bf16[2048,128]{1,0:T(8,128)(2,1)} %shard_map.168.refs_0_, bf16[512,128]{1,0:T(8,128)(2,1)S(1)} %add_convert_fusion.refs_1_, bf16[512,128]{1,0:T(8,128)(2,1)S(1)} %collective-permute-done.17.refs_2_, ...), custom_call_target="tpu_custom_call", output_to_operand_aliasing={{}: (0, {})} | custom-call | flops 1000000 | bytes 524288 | tf_op jit(solution)/shard_map/pallas_call | solution.py:216
  (4 shorter events, 0.1 us)
Async XLA Ops:
  3.4 1.5 %collective-permute-start.7 = (bf16[256,128]{1,0:T(8,128)(2,1)S(1)}, bf16[256,128]{1,0:T(8,128)(2,1)S(1)}, u32[]{:S(2)}, u32[]{:S(2)}) collective-permute-start(bf16[256,128]{1,0:T(8,128)(2,1)S(1)} %get-tuple-element.40.own_r), channel_id=1, source_target_pairs={{2,0},{3,1},{0,2},{1,3},{6,4},{7,5},{4,6},{5,7},{10,8},{11,9},{8,1... | collective-permute-start | bytes 196616 | tf_op jit(solution)/shard_map/ppermute | solution.py:604
  4.9 8.7 %collective-permute-start.8 = (bf16[512,128]{1,0:T(8,128)(2,1)S(1)}, bf16[512,128]{1,0:T(8,128)(2,1)S(1)}, u32[]{:S(2)}, u32[]{:S(2)}) collective-permute-start(bf16[512,128]{1,0:T(8,128)(2,1)S(1)} %pad_maximum_fusion), channel_id=1, source_target_pairs={{1,0},{5,1},{6,3},{0,4},{4,5},{3,6},{9,8},{13,9},{14,11},{8,12},{1... | collective-permute-start | bytes 393224 | tf_op jit(solution)/shard_map/ppermute | solution.py:604
  13.6 6.2 %collective-permute-start.9 = (bf16[512,128]{1,0:T(8,128)(2,1)S(1)}, bf16[512,128]{1,0:T(8,128)(2,1)S(1)}, u32[]{:S(2)}, u32[]{:S(2)}) collective-permute-start(bf16[512,128]{1,0:T(8,128)(2,1)S(1)} %collective-permute-done.8.got), channel_id=1, source_target_pairs={{2,0},{3,1},{0,2},{1,3},{6,4},{7,5},{4,6},{5,7},{10,8},{11,9},{8,1... | collective-permute-start | bytes 393224 | tf_op jit(solution)/shard_map/ppermute | solution.py:604
  14.4 5.4 %collective-permute-start.3 = (bf16[288,128]{1,0:T(8,128)(2,1)S(1)}, bf16[288,128]{1,0:T(8,128)(2,1)S(1)}, u32[]{:S(2)}, u32[]{:S(2)}) collective-permute-start(bf16[288,128]{1,0:T(8,128)(2,1)S(1)} %get-tuple-element.33.sent.left_own), channel_id=1, source_target_pairs={{1,0},{0,1},{3,2},{2,3},{5,4},{4,5},{7,6},{6,7},{9,8},{8,9},{11,10... | collective-permute-start | bytes 221192 | tf_op jit(solution)/shard_map/ppermute | solution.py:604
  16.8 6.2 %collective-permute-start.10 = (bf16[4,32,128]{2,1,0:T(8,128)(2,1)S(1)}, bf16[4,32,128]{2,1,0:T(8,128)(2,1)S(1)}, u32[]{:S(2)}, u32[]{:S(2)}) collective-permute-start(bf16[4,32,128]{2,1,0:T(8,128)(2,1)S(1)} %get-tuple-element.42.w_own), channel_id=1, source_target_pairs={{16,0},{17,1},{18,2},{19,3},{20,4},{21,5},{22,6},{23,7},{24,8},{25... | collective-permute-start | bytes 98312 | tf_op jit(solution)/shard_map/ppermute | solution.py:604
  23.0 2.6 %copy-start.2 = (bf16[256,64]{0,1:T(8,128)(2,1)S(1)}, bf16[256,64]{0,1:T(8,128)(2,1)}, u32[]{:S(2)}) copy-start(bf16[256,64]{0,1:T(8,128)(2,1)} %param.18) | copy-start | bytes 98308
  23.0 2.6 %copy-start.3 = (bf16[256,64]{0,1:T(8,128)(2,1)S(1)}, bf16[256,64]{0,1:T(8,128)(2,1)}, u32[]{:S(2)}) copy-start(bf16[256,64]{0,1:T(8,128)(2,1)} %param.19) | copy-start | bytes 98308
  23.0 2.6 %copy-start.4 = (bf16[256,64]{0,1:T(8,128)(2,1)S(1)}, bf16[256,64]{0,1:T(8,128)(2,1)}, u32[]{:S(2)}) copy-start(bf16[256,64]{0,1:T(8,128)(2,1)} %param.17) | copy-start | bytes 98308
  23.1 2.6 %copy-start.5 = (bf16[256,64]{0,1:T(8,128)(2,1)S(1)}, bf16[256,64]{0,1:T(8,128)(2,1)}, u32[]{:S(2)}) copy-start(bf16[256,64]{0,1:T(8,128)(2,1)} %param.20) | copy-start | bytes 98308
  23.8 9.2 %collective-permute-start.12 = (bf16[1024,128]{1,0:T(8,128)(2,1)S(1)}, bf16[1024,128]{1,0:T(8,128)(2,1)S(1)}, u32[]{:S(2)}, u32[]{:S(2)}) collective-permute-start(bf16[1024,128]{1,0:T(8,128)(2,1)S(1)} %shard_map.165.own), channel_id=1, source_target_pairs={{4,0},{5,1},{6,2},{7,3},{0,4},{1,5},{2,6},{3,7},{12,8},{13,9},{14,... | collective-permute-start | bytes 786440 | tf_op jit(solution)/shard_map/ppermute | solution.py:604
  26.1 11.5 %collective-permute-start.1 = (bf16[1024,128]{1,0:T(8,128)(2,1)S(1)}, bf16[1024,128]{1,0:T(8,128)(2,1)S(1)}, u32[]{:S(2)}, u32[]{:S(2)}) collective-permute-start(bf16[1024,128]{1,0:T(8,128)(2,1)S(1)} %get-tuple-element.28.own), channel_id=1, source_target_pairs={{4,0},{5,1},{6,2},{7,3},{0,4},{1,5},{2,6},{3,7},{12,8},{13,9},{14,... | collective-permute-start | bytes 786440 | tf_op jit(solution)/shard_map/ppermute | solution.py:604
  26.5 11.9 %collective-permute-start.11 = (bf16[1024,128]{1,0:T(8,128)(2,1)S(1)}, bf16[1024,128]{1,0:T(8,128)(2,1)S(1)}, u32[]{:S(2)}, u32[]{:S(2)}) collective-permute-start(bf16[1024,128]{1,0:T(8,128)(2,1)S(1)} %shard_map.165.own), channel_id=1, source_target_pairs={{2,0},{3,1},{0,2},{1,3},{6,4},{7,5},{4,6},{5,7},{10,8},{11,9},{8,1... | collective-permute-start | bytes 786440 | tf_op jit(solution)/shard_map/ppermute | solution.py:604
  33.0 5.3 %collective-permute-start.13 = (bf16[1024,128]{1,0:T(8,128)(2,1)S(1)}, bf16[1024,128]{1,0:T(8,128)(2,1)S(1)}, u32[]{:S(2)}, u32[]{:S(2)}) collective-permute-start(bf16[1024,128]{1,0:T(8,128)(2,1)S(1)} %collective-permute-done.12.across), channel_id=1, source_target_pairs={{2,0},{3,1},{0,2},{1,3},{6,4},{7,5},{4,6},{5,7},{10,8},{11,9},{8,1... | collective-permute-start | bytes 786440 | tf_op jit(solution)/shard_map/ppermute | solution.py:604
  33.0 7.6 %collective-permute-start = (bf16[1024,128]{1,0:T(8,128)(2,1)S(1)}, bf16[1024,128]{1,0:T(8,128)(2,1)S(1)}, u32[]{:S(2)}, u32[]{:S(2)}) collective-permute-start(bf16[1024,128]{1,0:T(8,128)(2,1)S(1)} %get-tuple-element.28.own), channel_id=1, source_target_pairs={{2,0},{3,1},{0,2},{1,3},{6,4},{7,5},{4,6},{5,7},{10,8},{11,9},{8,1... | collective-permute-start | bytes 786440 | tf_op jit(solution)/shard_map/ppermute | solution.py:604
  37.6 3.0 %collective-permute-start.2 = (bf16[1024,128]{1,0:T(8,128)(2,1)S(1)}, bf16[1024,128]{1,0:T(8,128)(2,1)S(1)}, u32[]{:S(2)}, u32[]{:S(2)}) collective-permute-start(bf16[1024,128]{1,0:T(8,128)(2,1)S(1)} %collective-permute-done.1.across), channel_id=1, source_target_pairs={{2,0},{3,1},{0,2},{1,3},{6,4},{7,5},{4,6},{5,7},{10,8},{11,9},{8,1... | collective-permute-start | bytes 786440 | tf_op jit(solution)/shard_map/ppermute | solution.py:604
  38.3 2.3 %copy-start.6 = (bf16[64,256]{1,0:T(8,128)(2,1)S(1)}, bf16[64,256]{1,0:T(8,128)(2,1)}, u32[]{:S(2)}) copy-start(bf16[64,256]{1,0:T(8,128)(2,1)} %w_out.1) | copy-start | bytes 98308
  39.1 9.1 %collective-permute-start.14 = (bf16[512,128]{1,0:T(8,128)(2,1)S(1)}, bf16[512,128]{1,0:T(8,128)(2,1)S(1)}, u32[]{:S(2)}, u32[]{:S(2)}) collective-permute-start(bf16[512,128]{1,0:T(8,128)(2,1)S(1)} %get-tuple-element.44), channel_id=1, source_target_pairs={{1,0},{0,1},{3,2},{2,3},{5,4},{4,5},{7,6},{6,7},{9,8},{8,9},{11,10... | collective-permute-start | bytes 393224 | tf_op jit(solution)/shard_map/ppermute | solution.py:604
  42.4 11.4 %collective-permute-start.4 = (bf16[512,128]{1,0:T(8,128)(2,1)S(1)}, bf16[512,128]{1,0:T(8,128)(2,1)S(1)}, u32[]{:S(2)}, u32[]{:S(2)}) collective-permute-start(bf16[512,128]{1,0:T(8,128)(2,1)S(1)} %get-tuple-element.35), channel_id=1, source_target_pairs={{8,0},{9,1},{10,2},{11,3},{12,4},{13,5},{14,6},{15,7},{0,8},{1,9},... | collective-permute-start | bytes 393224 | tf_op jit(solution)/shard_map/ppermute | solution.py:604
  44.0 12.9 %collective-permute-start.5 = (bf16[512,128]{1,0:T(8,128)(2,1)S(1)}, bf16[512,128]{1,0:T(8,128)(2,1)S(1)}, u32[]{:S(2)}, u32[]{:S(2)}) collective-permute-start(bf16[512,128]{1,0:T(8,128)(2,1)S(1)} %get-tuple-element.36), channel_id=1, source_target_pairs={{16,0},{17,1},{18,2},{19,3},{20,4},{21,5},{22,6},{23,7},{24,8},{25... | collective-permute-start | bytes 393224 | tf_op jit(solution)/shard_map/ppermute | solution.py:604
  46.6 10.4 %collective-permute-start.6 = (bf16[512,128]{1,0:T(8,128)(2,1)S(1)}, bf16[512,128]{1,0:T(8,128)(2,1)S(1)}, u32[]{:S(2)}, u32[]{:S(2)}) collective-permute-start(bf16[512,128]{1,0:T(8,128)(2,1)S(1)} %get-tuple-element.37), channel_id=1, source_target_pairs={{24,0},{25,1},{26,2},{27,3},{28,4},{29,5},{30,6},{31,7},{16,8},{17... | collective-permute-start | bytes 393224 | tf_op jit(solution)/shard_map/ppermute | solution.py:604
  47.6 5.0 %collective-permute-start.16 = (bf16[512,128]{1,0:T(8,128)(2,1)S(1)}, bf16[512,128]{1,0:T(8,128)(2,1)S(1)}, u32[]{:S(2)}, u32[]{:S(2)}) collective-permute-start(bf16[512,128]{1,0:T(8,128)(2,1)S(1)} %get-tuple-element.47), channel_id=1, source_target_pairs={{1,0},{0,1},{3,2},{2,3},{5,4},{4,5},{7,6},{6,7},{9,8},{8,9},{11,10... | collective-permute-start | bytes 393224 | tf_op jit(solution)/shard_map/ppermute | solution.py:604
  48.2 9.7 %collective-permute-start.15 = (bf16[512,128]{1,0:T(8,128)(2,1)S(1)}, bf16[512,128]{1,0:T(8,128)(2,1)S(1)}, u32[]{:S(2)}, u32[]{:S(2)}) collective-permute-start(bf16[512,128]{1,0:T(8,128)(2,1)S(1)} %add_convert_fusion.1.refs_0_), channel_id=1, source_target_pairs={{8,0},{9,1},{10,2},{11,3},{12,4},{13,5},{14,6},{15,7},{0,8},{1,9},... | collective-permute-start | bytes 393224 | tf_op jit(solution)/shard_map/ppermute | solution.py:604
  52.6 0.8 %copy-start.7 = (bf16[128,128]{1,0:T(8,128)(2,1)S(1)}, bf16[128,128]{1,0:T(8,128)(2,1)}, u32[]{:S(2)}) copy-start(bf16[128,128]{1,0:T(8,128)(2,1)} %close_w.1) | copy-start | bytes 98308
  52.6 4.3 %copy-start = (bf16[32,32,256]{2,1,0:T(8,128)(2,1)S(1)}, bf16[32,32,256]{2,1,0:T(8,128)(2,1)}, u32[]{:S(2)}) copy-start(bf16[32,32,256]{2,1,0:T(8,128)(2,1)} %param.15) | copy-start | bytes 1572868
  52.7 6.8 %collective-permute-start.17 = (bf16[512,128]{1,0:T(8,128)(2,1)S(1)}, bf16[512,128]{1,0:T(8,128)(2,1)S(1)}, u32[]{:S(2)}, u32[]{:S(2)}) collective-permute-start(bf16[512,128]{1,0:T(8,128)(2,1)S(1)} %add_convert_fusion.refs_1_), channel_id=1, source_target_pairs={{8,0},{9,1},{10,2},{11,3},{12,4},{13,5},{14,6},{15,7},{0,8},{1,9},... | collective-permute-start | bytes 393224 | tf_op jit(solution)/shard_map/ppermute | solution.py:604
  56.9 0.9 %copy-start.1 = (bf16[128,128]{1,0:T(8,128)(2,1)S(1)}, bf16[128,128]{1,0:T(8,128)(2,1)}, u32[]{:S(2)}) copy-start(bf16[128,128]{1,0:T(8,128)(2,1)} %refs_5_.1) | copy-start | bytes 98308
where the time goes:
time: 60.9 us; the launch traced here: 60.7 us
  waiting for transfers between devices  23 us (38%)
  starting transfers between devices  20.9 us (34%)
  Pallas kernels  15.8 us (26%)
  between operations  0.83 us (1%)
    ppermute x18, waiting for transfers between devices, send(): return lax.ppermute(x, AXES, pairs)  23 us
    ppermute x18, starting transfers between devices, send(): return lax.ppermute(x, AXES, pairs)  20.9 us
    pallas_call x13, Pallas kernels, run(): pl.pallas_call(body, out_shape=tuple((jax.ShapeDtypeStruct(s, d) for s, d...  15.8 us
  transfers between devices with their start and end apart: 18, of which 8 were waited for; matrix products, arithmetic and copies ran while one was open for 0% of the time, Pallas kernels for 18%

commit v1 on v0

--- a/solution.py
+++ b/solution.py
@@ -179,6 +179,7 @@
 LANES = 128
 HALF = LANES // 2
 QUART = LANES // 4
+PAD = 8
 
 
 def lane_of(shape):
@@ -257,7 +258,7 @@
         for s in range(step):
             piece = x[s * rows : (s + 1) * rows, :]
             for part in range(depth // LANES):
-                scr[part, pl.ds(first + s, rows, stride=share), :] = piece[
+                scr[part, pl.ds(first + s, rows, stride=share + PAD), :] = piece[
                     :, part * LANES : (part + 1) * LANES
                 ]
     moves[parts].wait()
@@ -265,9 +266,9 @@
     weights = jnp.concatenate([left_w[...], right_w[...]], axis=0)
     acc = 0
     for part in range(depth // LANES):
-        acc = acc + dot_nt(
-            weights[:, part * LANES : (part + 1) * LANES], scr[part].astype(BF16)
-        )
+        x = [scr[part, i * (share + PAD) : i * (share + PAD) + share, :] for i in range(rows)]
+        x = jnp.concatenate(x, axis=0).astype(BF16)
+        acc = acc + dot_nt(weights[:, part * LANES : (part + 1) * LANES], x)
     for g in range(n_rows // LANES):
         cut = slice(g * LANES, (g + 1) * LANES)
         left_t[g * width : (g + 1) * width, :] = acc[:width, cut].astype(BF16)
@@ -300,21 +301,24 @@
 def pair_body(width, couple, offset_t, outer_w, left_t, couple_t, message, outer_wt, scr, wscr):
     tiles = couple.shape[0] // LANES
     for t in range(tiles):
-        x = jnp.transpose(couple[t * LANES : (t + 1) * LANES, :].astype(F32))
-        couple_t[t] = x.astype(BF16)
+        x = jnp.transpose(couple[t * LANES : (t + 1) * LANES, :])
+        couple_t[t] = x
+        x = x.astype(F32)
         x = x - jnp.mean(x, axis=0, keepdims=True)
         x = x * lax.rsqrt(jnp.mean(x * x, axis=0, keepdims=True) + EPS)
         scr[pl.ds(t, offset_t.shape[0], stride=tiles), :] = dot_nn(offset_t[...], x.astype(BF16))
     span = left_t.shape[0]
     message[:span, :] = left_t[...]
     message[span:, :] = scr[...].astype(BF16)
-    wscr[...] = outer_w[...].astype(F32)
     per = LANES // width
+    for p in range(width):
+        cut = slice(p * width, (p + 1) * width)
+        wscr[p * (width + PAD) : p * (width + PAD) + width, :] = outer_w[cut, :].astype(F32)
     for g in range(width // per):
         block = jnp.concatenate(
-            [wscr[pl.ds(g * per + q, width, stride=width), :] for q in range(per)], axis=0
+            [wscr[pl.ds(g * per + q, width, stride=width + PAD), :] for q in range(per)], axis=0
         )
-        outer_wt[:, g * LANES : (g + 1) * LANES] = jnp.transpose(block).astype(BF16)
+        outer_wt[:, g * LANES : (g + 1) * LANES] = jnp.transpose(block.astype(BF16))
 
 
 def gate_tiles(scr, norm_t, w_own, w_far, first):
@@ -326,8 +330,14 @@
     for t in range(0, tiles, 2):
         y = dot_nn(weights, jnp.concatenate([norm_t[t], norm_t[t + 1]], axis=1))
         gated = jax.nn.sigmoid(y[half:]) * y[:half]
-        store_gated(scr, t, 2 * tiles, gated[:, :LANES])
-        store_gated(scr, t + 1, 2 * tiles, gated[:, LANES:])
+        store_gated(scr, t, 2 * tiles + PAD, gated[:, :LANES])
+        store_gated(scr, t + 1, 2 * tiles + PAD, gated[:, LANES:])
+
+
+def drop_pad(scr, out, rows):
+    for n in range(out.shape[0] // rows):
+        at = n * (rows + PAD)
+        out[n * rows : (n + 1) * rows, :] = scr[at : at + rows, :].astype(out.dtype)
 
 
 def store_gated(scr, t, rows, gated):
@@ -386,11 +396,12 @@
                     group == 0, roll(t0, -share * j4),
                     jnp.where(group == 1, roll(t1, share - share * j4), 0.0),
                 )
-                rscr[pl.ds(j, width, stride=2 * block), :] = tile
-                rscr[pl.ds(block + j, width, stride=2 * block), :] = roll(tile, HALF)
+                rscr[pl.ds(j, width, stride=2 * block + PAD), :] = tile
+                rscr[pl.ds(block + j, width, stride=2 * block + PAD), :] = roll(tile, HALF)
     left = lhs[...]
     for q in range(0, width, 2):
-        rhs = rscr[q * LANES : (q + 2) * LANES, :].astype(BF16)
+        at = [n * (LANES + PAD) for n in (q, q + 1)]
+        rhs = jnp.concatenate([rscr[n : n + LANES, :] for n in at], axis=0).astype(BF16)
         prod = dot_nt(left, rhs).astype(BF16)
         for t in range(tiles):
             for e in range(2):
@@ -411,12 +422,12 @@
 
 def right_body(norm_t, w_own, w_far, right_pk, gscr):
     gate_tiles(gscr, norm_t, w_own, w_far, 2)
-    right_pk[...] = gscr[...].astype(BF16)
+    drop_pad(gscr, right_pk, 2 * norm_t.shape[0])
 
 
 def left_body(norm_t, w_own, w_far, left_pk, gscr):
     gate_tiles(gscr, norm_t, w_own, w_far, 0)
-    left_pk[...] = gscr[...].astype(BF16)
+    drop_pad(gscr, left_pk, 2 * norm_t.shape[0])
 
 
 def close_body(norm_t, close_w, close_t):
@@ -459,8 +470,9 @@
     branch = lax.axis_index("branch")
     chans = half_own.shape[0] // n
     low = lane_of((chans, LANES)) < HALF
-    scr[0] = half_own[...].astype(F32)
-    scr[1] = half_far[...].astype(F32)
+    for h, half in enumerate((half_own, half_far)):
+        for c in range(chans):
+            scr[h, c * (n + PAD) : c * (n + PAD) + n, :] = half[c * n : (c + 1) * n, :].astype(F32)
     owners = [branch, branch ^ 2, branch ^ 1, branch ^ 3]
     w_t = [final_w[pl.ds(pl.multiple_of(o * chans, chans), chans), :] for o in owners]
     w_t = jnp.transpose(jnp.concatenate(w_t, axis=0).astype(F32)).astype(BF16)
@@ -468,23 +480,31 @@
     per = tiles // len(sems)
     base = part * tiles
     moves = []
-    for t in range(tiles):
+
+    def normed(t):
         blocks = []
         for h in range(2):
-            z0 = scr[h, pl.ds(2 * t, chans, stride=n), :]
-            z1 = scr[h, pl.ds(2 * t + 1, chans, stride=n), :]
+            z0 = scr[h, pl.ds(2 * t, chans, stride=n + PAD), :]
+            z1 = scr[h, pl.ds(2 * t + 1, chans, stride=n + PAD), :]
             blocks += [jnp.where(low, z0, roll(z1, HALF)), jnp.where(low, roll(z0, HALF), z1)]
         x = jnp.concatenate(blocks, axis=0)
         x = x - jnp.mean(x, axis=0, keepdims=True)
         x = x * lax.rsqrt(jnp.mean(x * x, axis=0, keepdims=True) + EPS)
-        change = dot_nn(w_t, x.astype(BF16))
-        result = mid_t[base + t].astype(F32) + close_t[base + t] * change
-        out[t * LANES : (t + 1) * LANES, :] = jnp.transpose(result).astype(BF16)
-        if t % per == per - 1:
-            here = out.at[pl.ds((t + 1 - per) * LANES, per * LANES)]
-            there = out_h.at[pl.ds((base + t + 1 - per) * LANES, per * LANES)]
-            moves.append(pltpu.make_async_copy(here, there, sems[t // per]))
-            moves[-1].start()
+        return x.astype(BF16)
+
+    for start in range(0, tiles, per):
+        change = dot_nn(
+            w_t, jnp.concatenate([normed(t) for t in range(start, start + per)], axis=1)
+        )
+        for e in range(per):
+            t = start + e
+            part_of = change[:, e * LANES : (e + 1) * LANES]
+            result = mid_t[base + t].astype(F32) + close_t[base + t] * part_of
+            out[t * LANES : (t + 1) * LANES, :] = jnp.transpose(result.astype(BF16))
+        here = out.at[pl.ds(start * LANES, per * LANES)]
+        there = out_h.at[pl.ds((base + start) * LANES, per * LANES)]
+        moves.append(pltpu.make_async_copy(here, there, sems[start // per]))
+        moves[-1].start()
     for move in moves:
         move.wait()
 
@@ -640,7 +660,7 @@
             ((local_heads, chans), BF16), ((4, quarter, chans), BF16),
         ],
         [
-            ((depth // LANES, n_rows, LANES), F32), ((n_rows, depth), BF16),
+            ((depth // LANES, rows * (share + PAD), LANES), F32), ((n_rows, depth), BF16),
             ((width, depth), BF16), ((width, depth), BF16),
         ],
         sems=9,
@@ -659,7 +679,7 @@
             ((flat[0] + local_heads * tiles, LANES), BF16),
             ((chans, width * width), BF16),
         ],
-        [((local_heads * tiles, LANES), F32), ((width * width, chans), F32)],
+        [((local_heads * tiles, LANES), F32), ((width * (width + PAD), chans), F32)],
     )(couple_v, offset_t, outer_w, left_t)
     got = send(message, other_col)
     kv, query, gate = call(
@@ -677,18 +697,18 @@
         [((tiles, chans, LANES), BF16), ((tiles, chans, LANES), BF16)],
         [
             ((tiles * width, LANES), BF16),
-            ((width * LANES, LANES), F32),
+            ((width * (LANES + PAD), LANES), F32),
             ((tiles, width * width, LANES), BF16),
         ],
         mib=16,
     )(couple_t, outer_wt, message, got, right_t, sib_r, got_r, got_rs)
     (right_pk,) = call(
-        right_body, [((quarter * rows, LANES), BF16)], [((quarter * rows, LANES), F32)]
+        right_body, [((quarter * rows, LANES), BF16)], [((quarter * (rows + PAD), LANES), F32)]
     )(norm_t, w_own, w_far)
     right_x = send(right_pk, other_chip)
     right_s = send(right_pk, other_core)
     (left_pk,) = call(
-        left_body, [((quarter * rows, LANES), BF16)], [((quarter * rows, LANES), F32)]
+        left_body, [((quarter * rows, LANES), BF16)], [((quarter * (rows + PAD), LANES), F32)]
     )(norm_t, w_own, w_far)
     parts = call(
         functools.partial(attend_body, rows, head),
@@ -716,9 +736,9 @@
         pair_out = call(
             functools.partial(final_body, rows // 2, part),
             [((rows * block, chans), BF16)],
-            [((2, quarter * rows // 2, LANES), F32), ((rows * block // 2, chans), BF16)],
+            [((2, quarter * (rows // 2 + PAD), LANES), F32), ((rows * block // 2, chans), BF16)],
             mib=12,
-            sems=2,
+            sems=4,
             out_hbm=1,
             anywhere=part,
             alias={0: 0} if part else None,

time: 60.9 us -> 58.5 us (0.961)
  Pallas kernels: 15.8 us -> 13.3 us
    pallas_call x13, Pallas kernels: 15.8 us -> 13.3 us  [run(): pl.pallas_call(body, out_shape=tuple((jax.ShapeDtypeStruct(s, d) for s, d...]
  transfers between devices with their start and end apart: 18 -> 18, of which waited for: 8 -> 8; matrix products, arithmetic and copies ran while one was open for 0% -> 0% of each run, Pallas kernels for 18% -> 16%
where the time goes in v1:
time: 58.5 us; the launch traced here: 58.2 us
  waiting for transfers between devices  23 us (39%)
  starting transfers between devices  21 us (36%)
  Pallas kernels  13.3 us (23%)
  between operations  0.82 us (1%)
    ppermute x18, waiting for transfers between devices, send(): return lax.ppermute(x, AXES, pairs)  23 us
    ppermute x18, starting transfers between devices, send(): return lax.ppermute(x, AXES, pairs)  21 us
    pallas_call x13, Pallas kernels, run(): pl.pallas_call(body, out_shape=tuple((jax.ShapeDtypeStruct(s, d) for s, d...  13.3 us
  transfers between devices with their start and end apart: 18, of which 8 were waited for; matrix products, arithmetic and copies ran while one was open for 0% of the time, Pallas kernels for 16%

profile of v1, /device:TPU:0, one launch (start us, length us, event | category | flops | bytes accessed | tf_op | source)
XLA Modules:
  0.0 58.2 jit_solution(2770759319670297707)
XLA Ops:
  0.6 2.2 %shard_map.158 = (bf16[1024,256]{1,0:T(8,128)(2,1)S(1)}, bf16[256,128]{1,0:T(8,128)(2,1)S(1)}, bf16[256,128]{1,0:T(8,128)(2,1)S(1)}, bf16[2048,128]{1,0:T(8,128)...) custom-call(bf16[1024,256]{1,0:T(8,128)(2,1)} %bitcast.13, ...), custom_call_target="tpu_custom_call" | custom-call | flops 1000000 | bytes 524288 | tf_op jit(solution)/shard_map/pallas_call | solution.py:217
  2.8 0.6 collective-permute-start.7
  3.4 0.9 %collective-permute-done.7.sib_r = bf16[256,128]{1,0:T(8,128)(2,1)S(1)} collective-permute-done((bf16[256,128]{1,0:T(8,128)(2,1)S(1)}, bf16[256,128]{1,0:T(8,128)(2,1)S(1)}, u32[]{:S(2)}, u32[]{:S(2)}) %collective-permute-start.7) | collective-permute-done | bytes 65568 | tf_op jit(solution)/shard_map/ppermute | solution.py:624
  4.3 4.8 %collective-permute-start.8 = (bf16[512,128]{1,0:T(8,128)(2,1)S(1)}, bf16[512,128]{1,0:T(8,128)(2,1)S(1)}, u32[]{:S(2)}, u32[]{:S(2)}) collective-permute-start(bf16[512,128]{1,0:T(8,128)(2,1)S(1)} %pad_maximum_fusion), channel_id=1, source_target_pairs={{1,0},{5,1},{6,3},{0,4},{4,5},{3,6},{9,8},{13,9},{14,11},{8,12},{1... | collective-permute-start | bytes 393224 | tf_op jit(solution)/shard_map/ppermute | solution.py:624
  9.1 3.9 %collective-permute-done.8.got = bf16[512,128]{1,0:T(8,128)(2,1)S(1)} collective-permute-done((bf16[512,128]{1,0:T(8,128)(2,1)S(1)}, bf16[512,128]{1,0:T(8,128)(2,1)S(1)}, u32[]{:S(2)}, u32[]{:S(2)}) %collective-permute-start.8) | collective-permute-done | bytes 131104 | tf_op jit(solution)/shard_map/ppermute | solution.py:624
  13.0 0.0 collective-permute-start.9
  13.0 0.6 %shard_map.160 = (bf16[16,128,128]{2,1,0:T(8,128)(2,1)S(1)}, bf16[288,128]{1,0:T(8,128)(2,1)S(1)}, bf16[128,1024]{1,0:T(8,128)(2,1)S(1)}) custom-call(bf16[2048,128]{1,0:T(8,128)(2,1)S(1)} %get-tuple-element.29.couple, bf16[2,128]{1,0:T(2,128)(2,1)S(1)} %get-tuple-element.30.offset_t, bf16[1024,128]{1,0:T(8,128)(2,1)S(1)} %get-tuple-element.31.outer_w, ...), custom_call_target="tpu_custom_call" | custom-call | flops 1000000 | bytes 524288 | tf_op jit(solution)/shard_map/pallas_call | solution.py:217
  13.6 2.5 %collective-permute-start.3 = (bf16[288,128]{1,0:T(8,128)(2,1)S(1)}, bf16[288,128]{1,0:T(8,128)(2,1)S(1)}, u32[]{:S(2)}, u32[]{:S(2)}) collective-permute-start(bf16[288,128]{1,0:T(8,128)(2,1)S(1)} %get-tuple-element.33.sent.left_own), channel_id=1, source_target_pairs={{1,0},{0,1},{3,2},{2,3},{5,4},{4,5},{7,6},{6,7},{9,8},{8,9},{11,10... | collective-permute-start | bytes 221192 | tf_op jit(solution)/shard_map/ppermute | solution.py:624
  16.0 2.6 %collective-permute-start.10 = (bf16[4,32,128]{2,1,0:T(8,128)(2,1)S(1)}, bf16[4,32,128]{2,1,0:T(8,128)(2,1)S(1)}, u32[]{:S(2)}, u32[]{:S(2)}) collective-permute-start(bf16[4,32,128]{2,1,0:T(8,128)(2,1)S(1)} %get-tuple-element.42.w_own), channel_id=1, source_target_pairs={{16,0},{17,1},{18,2},{19,3},{20,4},{21,5},{22,6},{23,7},{24,8},{25... | collective-permute-start | bytes 98312 | tf_op jit(solution)/shard_map/ppermute | solution.py:624
  18.6 0.3 collective-permute-done.3.got.left_far
  19.0 0.0 collective-permute-done.9.got_sib
  19.0 2.2 %shard_map.163 = (bf16[16,128,128]{2,1,0:T(8,128)(2,1)S(1)}, bf16[16,128,128]{2,1,0:T(8,128)(2,1)S(1)}) custom-call(bf16[16,128,128]{2,1,0:T(8,128)(2,1)S(1)} %get-tuple-element.38.couple_t, bf16[128,1024]{1,0:T(8,128)(2,1)S(1)} %get-tuple-element.39.outer_wt, bf16[288,128]{1,0:T(8,128)(2,1)S(1)} %get-tuple-element.33.sent.left_own, ...), custom_call_target="tpu_custom_call" | custom-call | flops 1000000 | bytes 524288 | tf_op jit(solution)/shard_map/pallas_call | solution.py:217
  21.2 0.0 collective-permute-done.10.w_far
  21.2 0.0 copy-start.2
  21.2 0.0 copy-start.3
  21.3 0.0 copy-start.4
  21.3 0.0 copy-start.5
  21.3 0.4 shard_map.165.own
  21.7 1.8 %collective-permute-start.12 = (bf16[1024,128]{1,0:T(8,128)(2,1)S(1)}, bf16[1024,128]{1,0:T(8,128)(2,1)S(1)}, u32[]{:S(2)}, u32[]{:S(2)}) collective-permute-start(bf16[1024,128]{1,0:T(8,128)(2,1)S(1)} %shard_map.165.own), channel_id=1, source_target_pairs={{4,0},{5,1},{6,2},{7,3},{0,4},{1,5},{2,6},{3,7},{12,8},{13,9},{14,... | collective-permute-start | bytes 786440 | tf_op jit(solution)/shard_map/ppermute | solution.py:624
  23.5 0.0 copy-done.2
  23.5 0.0 copy-done.3
  23.5 0.0 copy-done.4
  23.5 0.0 copy-done.5
  23.5 0.5 shard_map.159
  24.1 0.3 collective-permute-start.1
  24.4 0.0 collective-permute-start.11
  24.4 6.5 %collective-permute-done.12.across = bf16[1024,128]{1,0:T(8,128)(2,1)S(1)} collective-permute-done((bf16[1024,128]{1,0:T(8,128)(2,1)S(1)}, bf16[1024,128]{1,0:T(8,128)(2,1)S(1)}, u32[]{:S(2)}, u32[]{:S(2)}) %collective-permute-start.12) | collective-permute-done | bytes 262176 | tf_op jit(solution)/shard_map/ppermute | solution.py:624
  30.9 0.0 collective-permute-start.13
  30.9 0.5 collective-permute-start
  31.4 4.1 %collective-permute-done.1.across = bf16[1024,128]{1,0:T(8,128)(2,1)S(1)} collective-permute-done((bf16[1024,128]{1,0:T(8,128)(2,1)S(1)}, bf16[1024,128]{1,0:T(8,128)(2,1)S(1)}, u32[]{:S(2)}, u32[]{:S(2)}) %collective-permute-start.1) | collective-permute-done | bytes 262176 | tf_op jit(solution)/shard_map/ppermute | solution.py:624
  35.5 0.0 collective-permute-start.2
  35.5 0.4 shard_map.164.left_pk
  35.9 0.0 copy-start.6
  35.9 0.0 collective-permute-done.11.sib
  36.0 0.0 collective-permute-done.13.across_sib
  36.0 0.8 %shard_map.166 = (f32[512,128]{1,0:T(8,128)S(1)}, bf16[512,128]{1,0:T(8,128)(2,1)S(1)}) custom-call(bf16[1024,128]{1,0:T(8,128)(2,1)S(1)} %shard_map.164.left_pk, bf16[1024,128]{1,0:T(8,128)(2,1)S(1)} %shard_map.165.own, bf16[1024,128]{1,0:T(8,128)(2,1)S(1)} %collective-permute-done.11.sib, bf16[1024,128]{1,0:T(8,128)(2,1)S(1)} %collective-permute-done.12.across, ...), custom_call_target="tpu_custom_call" | custom-call | flops 1000000 | bytes 524288 | tf_op jit(solution)/shard_map/pallas_call | solution.py:217
  36.7 1.5 %collective-permute-start.14 = (bf16[512,128]{1,0:T(8,128)(2,1)S(1)}, bf16[512,128]{1,0:T(8,128)(2,1)S(1)}, u32[]{:S(2)}, u32[]{:S(2)}) collective-permute-start(bf16[512,128]{1,0:T(8,128)(2,1)S(1)} %get-tuple-element.44), channel_id=1, source_target_pairs={{1,0},{0,1},{3,2},{2,3},{5,4},{4,5},{7,6},{6,7},{9,8},{8,9},{11,10... | collective-permute-start | bytes 393224 | tf_op jit(solution)/shard_map/ppermute | solution.py:624
  38.2 0.0 collective-permute-done.sib
  38.2 0.0 collective-permute-done.2.across_sib
  38.2 0.0 copy-done.6
  38.3 1.7 %shard_map.161 = (bf16[512,128]{1,0:T(8,128)(2,1)S(1)}, bf16[512,128]{1,0:T(8,128)(2,1)S(1)}, bf16[512,128]{1,0:T(8,128)(2,1)S(1)}, bf16[512,128]{1,0:T(8,128)(2,1)S(1)}) custom-call(bf16[512,128]{1,0:T(8,128)(2,1)S(1)} %get-tuple-element.26.query, f32[512,128]{1,0:T(8,128)S(1)} %get-tuple-element.27.gate, bf16[1024,128]{1,0:T(8,128)(2,1)S(1)} %get-tuple-element.28.own, ...), custom_call_target="tpu_custom_call" | custom-call | flops 1000000 | bytes 524288 | tf_op jit(solution)/shard_map/pallas_call | solution.py:217
  40.0 1.6 %collective-permute-start.4 = (bf16[512,128]{1,0:T(8,128)(2,1)S(1)}, bf16[512,128]{1,0:T(8,128)(2,1)S(1)}, u32[]{:S(2)}, u32[]{:S(2)}) collective-permute-start(bf16[512,128]{1,0:T(8,128)(2,1)S(1)} %get-tuple-element.35), channel_id=1, source_target_pairs={{8,0},{9,1},{10,2},{11,3},{12,4},{13,5},{14,6},{15,7},{0,8},{1,9},... | collective-permute-start | bytes 393224 | tf_op jit(solution)/shard_map/ppermute | solution.py:624
  41.6 2.6 %collective-permute-start.5 = (bf16[512,128]{1,0:T(8,128)(2,1)S(1)}, bf16[512,128]{1,0:T(8,128)(2,1)S(1)}, u32[]{:S(2)}, u32[]{:S(2)}) collective-permute-start(bf16[512,128]{1,0:T(8,128)(2,1)S(1)} %get-tuple-element.36), channel_id=1, source_target_pairs={{16,0},{17,1},{18,2},{19,3},{20,4},{21,5},{22,6},{23,7},{24,8},{25... | collective-permute-start | bytes 393224 | tf_op jit(solution)/shard_map/ppermute | solution.py:624
  44.2 0.2 collective-permute-start.6
  44.4 0.7 %shard_map.169 = (f32[512,128]{1,0:T(8,128)S(1)}, bf16[512,128]{1,0:T(8,128)(2,1)S(1)}) custom-call(bf16[1024,128]{1,0:T(8,128)(2,1)S(1)} %shard_map.164.left_pk, bf16[1024,128]{1,0:T(8,128)(2,1)S(1)} %shard_map.165.own, bf16[1024,128]{1,0:T(8,128)(2,1)S(1)} %collective-permute-done.11.sib, bf16[1024,128]{1,0:T(8,128)(2,1)S(1)} %collective-permute-done.12.across, ...), custom_call_target="tpu_custom_call" | custom-call | flops 1000000 | bytes 524288 | tf_op jit(solution)/shard_map/pallas_call | solution.py:217
  45.2 0.6 %collective-permute-start.16 = (bf16[512,128]{1,0:T(8,128)(2,1)S(1)}, bf16[512,128]{1,0:T(8,128)(2,1)S(1)}, u32[]{:S(2)}, u32[]{:S(2)}) collective-permute-start(bf16[512,128]{1,0:T(8,128)(2,1)S(1)} %get-tuple-element.47), channel_id=1, source_target_pairs={{1,0},{0,1},{3,2},{2,3},{5,4},{4,5},{7,6},{6,7},{9,8},{8,9},{11,10... | collective-permute-start | bytes 393224 | tf_op jit(solution)/shard_map/ppermute | solution.py:624
  45.8 0.0 collective-permute-done.14
  45.8 0.6 collective-permute-start.15
  46.4 3.8 %collective-permute-done.16 = bf16[512,128]{1,0:T(8,128)(2,1)S(1)} collective-permute-done((bf16[512,128]{1,0:T(8,128)(2,1)S(1)}, bf16[512,128]{1,0:T(8,128)(2,1)S(1)}, u32[]{:S(2)}, u32[]{:S(2)}) %collective-permute-start.16) | collective-permute-done | bytes 131104 | tf_op jit(solution)/shard_map/ppermute | solution.py:624
  50.2 0.0 copy-start.7
  50.2 0.0 copy-start
  50.3 0.7 %collective-permute-start.17 = (bf16[512,128]{1,0:T(8,128)(2,1)S(1)}, bf16[512,128]{1,0:T(8,128)(2,1)S(1)}, u32[]{:S(2)}, u32[]{:S(2)}) collective-permute-start(bf16[512,128]{1,0:T(8,128)(2,1)S(1)} %add_convert_fusion.refs_1_), channel_id=1, source_target_pairs={{8,0},{9,1},{10,2},{11,3},{12,4},{13,5},{14,6},{15,7},{0,8},{1,9},... | collective-permute-start | bytes 393224 | tf_op jit(solution)/shard_map/ppermute | solution.py:624
  51.0 0.0 copy-done.7
  51.0 0.4 shard_map.167.refs_3_.refs_4_
  51.4 0.0 collective-permute-done.4.p1
  51.4 3.1 %collective-permute-done.5.p2 = bf16[512,128]{1,0:T(8,128)(2,1)S(1)} collective-permute-done((bf16[512,128]{1,0:T(8,128)(2,1)S(1)}, bf16[512,128]{1,0:T(8,128)(2,1)S(1)}, u32[]{:S(2)}, u32[]{:S(2)}) %collective-permute-start.5) | collective-permute-done | bytes 131104 | tf_op jit(solution)/shard_map/ppermute | solution.py:624
  54.5 0.0 collective-permute-done.6.p3
  54.5 0.0 copy-done
  54.5 0.9 %shard_map.162 = bf16[1024,64]{1,0:T(8,128)(2,1)} custom-call(bf16[1024,256]{1,0:T(8,128)(2,1)S(1)} %bitcast.14, bf16[512,128]{1,0:T(8,128)(2,1)S(1)} %get-tuple-element.34.p0, bf16[512,128]{1,0:T(8,128)(2,1)S(1)} %collective-permute-done.4.p1, bf16[512,128]{1,0:T(8,128)(2,1)S(1)} %collective-permute-done.5.p2, bf16[512,128]{1,0:T(8,128)(2,1)S(1)} %collective-permute-done.6.p3), custom_call_target="tpu_custom_call" | custom-call | flops 1000000 | bytes 524288 | tf_op jit(solution)/shard_map/pallas_call | solution.py:217
  55.5 0.0 collective-permute-done.15.refs_1_
  55.5 0.0 copy-done.1
  55.5 1.2 %shard_map.168.refs_0_ = bf16[2048,128]{1,0:T(8,128)(2,1)} custom-call(bf16[512,128]{1,0:T(8,128)(2,1)S(1)} %add_convert_fusion.1.refs_0_, bf16[512,128]{1,0:T(8,128)(2,1)S(1)} %collective-permute-done.15.refs_1_, bf16[16,128,128]{2,1,0:T(8,128)(2,1)S(1)} %get-tuple-element.45.refs_2_.refs_3_, f32[16,128,128]{2,1,0:T(8,128)S(1)} %shard_map.167.refs_3_.refs_4_, ...), custom_call_target="tpu_custom_call" | custom-call | flops 1000000 | bytes 524288 | tf_op jit(solution)/shard_map/pallas_call | solution.py:217
  56.7 0.3 collective-permute-done.17.refs_2_
  57.0 1.2 %shard_map.170 = bf16[2048,128]{1,0:T(8,128)(2,1)} custom-call(bf16[2048,128]{1,0:T(8,128)(2,1)} %shard_map.168.refs_0_, bf16[512,128]{1,0:T(8,128)(2,1)S(1)} %add_convert_fusion.refs_1_, bf16[512,128]{1,0:T(8,128)(2,1)S(1)} %collective-permute-done.17.refs_2_, ...), custom_call_target="tpu_custom_call", output_to_operand_aliasing={{}: (0, {})} | custom-call | flops 1000000 | bytes 524288 | tf_op jit(solution)/shard_map/pallas_call | solution.py:217
  (4 shorter events, 0.1 us)
Async XLA Ops:
  2.8 1.5 %collective-permute-start.7 = (bf16[256,128]{1,0:T(8,128)(2,1)S(1)}, bf16[256,128]{1,0:T(8,128)(2,1)S(1)}, u32[]{:S(2)}, u32[]{:S(2)}) collective-permute-start(bf16[256,128]{1,0:T(8,128)(2,1)S(1)} %get-tuple-element.40.own_r), channel_id=1, source_target_pairs={{2,0},{3,1},{0,2},{1,3},{6,4},{7,5},{4,6},{5,7},{10,8},{11,9},{8,1... | collective-permute-start | bytes 196616 | tf_op jit(solution)/shard_map/ppermute | solution.py:624
  4.3 8.7 %collective-permute-start.8 = (bf16[512,128]{1,0:T(8,128)(2,1)S(1)}, bf16[512,128]{1,0:T(8,128)(2,1)S(1)}, u32[]{:S(2)}, u32[]{:S(2)}) collective-permute-start(bf16[512,128]{1,0:T(8,128)(2,1)S(1)} %pad_maximum_fusion), channel_id=1, source_target_pairs={{1,0},{5,1},{6,3},{0,4},{4,5},{3,6},{9,8},{13,9},{14,11},{8,12},{1... | collective-permute-start | bytes 393224 | tf_op jit(solution)/shard_map/ppermute | solution.py:624
  13.0 6.0 %collective-permute-start.9 = (bf16[512,128]{1,0:T(8,128)(2,1)S(1)}, bf16[512,128]{1,0:T(8,128)(2,1)S(1)}, u32[]{:S(2)}, u32[]{:S(2)}) collective-permute-start(bf16[512,128]{1,0:T(8,128)(2,1)S(1)} %collective-permute-done.8.got), channel_id=1, source_target_pairs={{2,0},{3,1},{0,2},{1,3},{6,4},{7,5},{4,6},{5,7},{10,8},{11,9},{8,1... | collective-permute-start | bytes 393224 | tf_op jit(solution)/shard_map/ppermute | solution.py:624
  13.6 5.4 %collective-permute-start.3 = (bf16[288,128]{1,0:T(8,128)(2,1)S(1)}, bf16[288,128]{1,0:T(8,128)(2,1)S(1)}, u32[]{:S(2)}, u32[]{:S(2)}) collective-permute-start(bf16[288,128]{1,0:T(8,128)(2,1)S(1)} %get-tuple-element.33.sent.left_own), channel_id=1, source_target_pairs={{1,0},{0,1},{3,2},{2,3},{5,4},{4,5},{7,6},{6,7},{9,8},{8,9},{11,10... | collective-permute-start | bytes 221192 | tf_op jit(solution)/shard_map/ppermute | solution.py:624
  16.0 5.2 %collective-permute-start.10 = (bf16[4,32,128]{2,1,0:T(8,128)(2,1)S(1)}, bf16[4,32,128]{2,1,0:T(8,128)(2,1)S(1)}, u32[]{:S(2)}, u32[]{:S(2)}) collective-permute-start(bf16[4,32,128]{2,1,0:T(8,128)(2,1)S(1)} %get-tuple-element.42.w_own), channel_id=1, source_target_pairs={{16,0},{17,1},{18,2},{19,3},{20,4},{21,5},{22,6},{23,7},{24,8},{25... | collective-permute-start | bytes 98312 | tf_op jit(solution)/shard_map/ppermute | solution.py:624
  21.2 2.3 %copy-start.2 = (bf16[256,64]{0,1:T(8,128)(2,1)S(1)}, bf16[256,64]{0,1:T(8,128)(2,1)}, u32[]{:S(2)}) copy-start(bf16[256,64]{0,1:T(8,128)(2,1)} %param.18) | copy-start | bytes 98308
  21.2 2.3 %copy-start.3 = (bf16[256,64]{0,1:T(8,128)(2,1)S(1)}, bf16[256,64]{0,1:T(8,128)(2,1)}, u32[]{:S(2)}) copy-start(bf16[256,64]{0,1:T(8,128)(2,1)} %param.19) | copy-start | bytes 98308
  21.3 2.3 %copy-start.4 = (bf16[256,64]{0,1:T(8,128)(2,1)S(1)}, bf16[256,64]{0,1:T(8,128)(2,1)}, u32[]{:S(2)}) copy-start(bf16[256,64]{0,1:T(8,128)(2,1)} %param.17) | copy-start | bytes 98308
  21.3 2.3 %copy-start.5 = (bf16[256,64]{0,1:T(8,128)(2,1)S(1)}, bf16[256,64]{0,1:T(8,128)(2,1)}, u32[]{:S(2)}) copy-start(bf16[256,64]{0,1:T(8,128)(2,1)} %param.20) | copy-start | bytes 98308
  21.7 9.2 %collective-permute-start.12 = (bf16[1024,128]{1,0:T(8,128)(2,1)S(1)}, bf16[1024,128]{1,0:T(8,128)(2,1)S(1)}, u32[]{:S(2)}, u32[]{:S(2)}) collective-permute-start(bf16[1024,128]{1,0:T(8,128)(2,1)S(1)} %shard_map.165.own), channel_id=1, source_target_pairs={{4,0},{5,1},{6,2},{7,3},{0,4},{1,5},{2,6},{3,7},{12,8},{13,9},{14,... | collective-permute-start | bytes 786440 | tf_op jit(solution)/shard_map/ppermute | solution.py:624
  24.1 11.5 %collective-permute-start.1 = (bf16[1024,128]{1,0:T(8,128)(2,1)S(1)}, bf16[1024,128]{1,0:T(8,128)(2,1)S(1)}, u32[]{:S(2)}, u32[]{:S(2)}) collective-permute-start(bf16[1024,128]{1,0:T(8,128)(2,1)S(1)} %get-tuple-element.28.own), channel_id=1, source_target_pairs={{4,0},{5,1},{6,2},{7,3},{0,4},{1,5},{2,6},{3,7},{12,8},{13,9},{14,... | collective-permute-start | bytes 786440 | tf_op jit(solution)/shard_map/ppermute | solution.py:624
  24.4 11.6 %collective-permute-start.11 = (bf16[1024,128]{1,0:T(8,128)(2,1)S(1)}, bf16[1024,128]{1,0:T(8,128)(2,1)S(1)}, u32[]{:S(2)}, u32[]{:S(2)}) collective-permute-start(bf16[1024,128]{1,0:T(8,128)(2,1)S(1)} %shard_map.165.own), channel_id=1, source_target_pairs={{2,0},{3,1},{0,2},{1,3},{6,4},{7,5},{4,6},{5,7},{10,8},{11,9},{8,1... | collective-permute-start | bytes 786440 | tf_op jit(solution)/shard_map/ppermute | solution.py:624
  30.9 5.0 %collective-permute-start.13 = (bf16[1024,128]{1,0:T(8,128)(2,1)S(1)}, bf16[1024,128]{1,0:T(8,128)(2,1)S(1)}, u32[]{:S(2)}, u32[]{:S(2)}) collective-permute-start(bf16[1024,128]{1,0:T(8,128)(2,1)S(1)} %collective-permute-done.12.across), channel_id=1, source_target_pairs={{2,0},{3,1},{0,2},{1,3},{6,4},{7,5},{4,6},{5,7},{10,8},{11,9},{8,1... | collective-permute-start | bytes 786440 | tf_op jit(solution)/shard_map/ppermute | solution.py:624
  30.9 7.3 %collective-permute-start = (bf16[1024,128]{1,0:T(8,128)(2,1)S(1)}, bf16[1024,128]{1,0:T(8,128)(2,1)S(1)}, u32[]{:S(2)}, u32[]{:S(2)}) collective-permute-start(bf16[1024,128]{1,0:T(8,128)(2,1)S(1)} %get-tuple-element.28.own), channel_id=1, source_target_pairs={{2,0},{3,1},{0,2},{1,3},{6,4},{7,5},{4,6},{5,7},{10,8},{11,9},{8,1... | collective-permute-start | bytes 786440 | tf_op jit(solution)/shard_map/ppermute | solution.py:624
  35.5 2.7 %collective-permute-start.2 = (bf16[1024,128]{1,0:T(8,128)(2,1)S(1)}, bf16[1024,128]{1,0:T(8,128)(2,1)S(1)}, u32[]{:S(2)}, u32[]{:S(2)}) collective-permute-start(bf16[1024,128]{1,0:T(8,128)(2,1)S(1)} %collective-permute-done.1.across), channel_id=1, source_target_pairs={{2,0},{3,1},{0,2},{1,3},{6,4},{7,5},{4,6},{5,7},{10,8},{11,9},{8,1... | collective-permute-start | bytes 786440 | tf_op jit(solution)/shard_map/ppermute | solution.py:624
  35.9 2.3 %copy-start.6 = (bf16[64,256]{1,0:T(8,128)(2,1)S(1)}, bf16[64,256]{1,0:T(8,128)(2,1)}, u32[]{:S(2)}) copy-start(bf16[64,256]{1,0:T(8,128)(2,1)} %w_out.1) | copy-start | bytes 98308
  36.7 9.1 %collective-permute-start.14 = (bf16[512,128]{1,0:T(8,128)(2,1)S(1)}, bf16[512,128]{1,0:T(8,128)(2,1)S(1)}, u32[]{:S(2)}, u32[]{:S(2)}) collective-permute-start(bf16[512,128]{1,0:T(8,128)(2,1)S(1)} %get-tuple-element.44), channel_id=1, source_target_pairs={{1,0},{0,1},{3,2},{2,3},{5,4},{4,5},{7,6},{6,7},{9,8},{8,9},{11,10... | collective-permute-start | bytes 393224 | tf_op jit(solution)/shard_map/ppermute | solution.py:624
  40.0 11.4 %collective-permute-start.4 = (bf16[512,128]{1,0:T(8,128)(2,1)S(1)}, bf16[512,128]{1,0:T(8,128)(2,1)S(1)}, u32[]{:S(2)}, u32[]{:S(2)}) collective-permute-start(bf16[512,128]{1,0:T(8,128)(2,1)S(1)} %get-tuple-element.35), channel_id=1, source_target_pairs={{8,0},{9,1},{10,2},{11,3},{12,4},{13,5},{14,6},{15,7},{0,8},{1,9},... | collective-permute-start | bytes 393224 | tf_op jit(solution)/shard_map/ppermute | solution.py:624
  41.6 12.9 %collective-permute-start.5 = (bf16[512,128]{1,0:T(8,128)(2,1)S(1)}, bf16[512,128]{1,0:T(8,128)(2,1)S(1)}, u32[]{:S(2)}, u32[]{:S(2)}) collective-permute-start(bf16[512,128]{1,0:T(8,128)(2,1)S(1)} %get-tuple-element.36), channel_id=1, source_target_pairs={{16,0},{17,1},{18,2},{19,3},{20,4},{21,5},{22,6},{23,7},{24,8},{25... | collective-permute-start | bytes 393224 | tf_op jit(solution)/shard_map/ppermute | solution.py:624
  44.2 10.3 %collective-permute-start.6 = (bf16[512,128]{1,0:T(8,128)(2,1)S(1)}, bf16[512,128]{1,0:T(8,128)(2,1)S(1)}, u32[]{:S(2)}, u32[]{:S(2)}) collective-permute-start(bf16[512,128]{1,0:T(8,128)(2,1)S(1)} %get-tuple-element.37), channel_id=1, source_target_pairs={{24,0},{25,1},{26,2},{27,3},{28,4},{29,5},{30,6},{31,7},{16,8},{17... | collective-permute-start | bytes 393224 | tf_op jit(solution)/shard_map/ppermute | solution.py:624
  45.2 5.0 %collective-permute-start.16 = (bf16[512,128]{1,0:T(8,128)(2,1)S(1)}, bf16[512,128]{1,0:T(8,128)(2,1)S(1)}, u32[]{:S(2)}, u32[]{:S(2)}) collective-permute-start(bf16[512,128]{1,0:T(8,128)(2,1)S(1)} %get-tuple-element.47), channel_id=1, source_target_pairs={{1,0},{0,1},{3,2},{2,3},{5,4},{4,5},{7,6},{6,7},{9,8},{8,9},{11,10... | collective-permute-start | bytes 393224 | tf_op jit(solution)/shard_map/ppermute | solution.py:624
  45.8 9.7 %collective-permute-start.15 = (bf16[512,128]{1,0:T(8,128)(2,1)S(1)}, bf16[512,128]{1,0:T(8,128)(2,1)S(1)}, u32[]{:S(2)}, u32[]{:S(2)}) collective-permute-start(bf16[512,128]{1,0:T(8,128)(2,1)S(1)} %add_convert_fusion.1.refs_0_), channel_id=1, source_target_pairs={{8,0},{9,1},{10,2},{11,3},{12,4},{13,5},{14,6},{15,7},{0,8},{1,9},... | collective-permute-start | bytes 393224 | tf_op jit(solution)/shard_map/ppermute | solution.py:624
  50.2 0.8 %copy-start.7 = (bf16[128,128]{1,0:T(8,128)(2,1)S(1)}, bf16[128,128]{1,0:T(8,128)(2,1)}, u32[]{:S(2)}) copy-start(bf16[128,128]{1,0:T(8,128)(2,1)} %close_w.1) | copy-start | bytes 98308
  50.2 4.3 %copy-start = (bf16[32,32,256]{2,1,0:T(8,128)(2,1)S(1)}, bf16[32,32,256]{2,1,0:T(8,128)(2,1)}, u32[]{:S(2)}) copy-start(bf16[32,32,256]{2,1,0:T(8,128)(2,1)} %param.15) | copy-start | bytes 1572868
  50.3 6.8 %collective-permute-start.17 = (bf16[512,128]{1,0:T(8,128)(2,1)S(1)}, bf16[512,128]{1,0:T(8,128)(2,1)S(1)}, u32[]{:S(2)}, u32[]{:S(2)}) collective-permute-start(bf16[512,128]{1,0:T(8,128)(2,1)S(1)} %add_convert_fusion.refs_1_), channel_id=1, source_target_pairs={{8,0},{9,1},{10,2},{11,3},{12,4},{13,5},{14,6},{15,7},{0,8},{1,9},... | collective-permute-start | bytes 393224 | tf_op jit(solution)/shard_map/ppermute | solution.py:624
  54.5 0.9 %copy-start.1 = (bf16[128,128]{1,0:T(8,128)(2,1)S(1)}, bf16[128,128]{1,0:T(8,128)(2,1)}, u32[]{:S(2)}) copy-start(bf16[128,128]{1,0:T(8,128)(2,1)} %refs_5_.1) | copy-start | bytes 98308

commit v2 on v1

--- a/solution.py
+++ b/solution.py
@@ -282,18 +282,20 @@
     x = normed[...]
     low = lane_of((half, LANES)) < HALF
 
-    def both(w0, w1):
-        y = dot_nt(x, jnp.concatenate([w0[...], w1[...]], axis=0))
+    weights = [w[...] for w in (key_w, value_w, query_w, gate_w)]
+    full = dot_nt(x, jnp.concatenate(weights, axis=0))
+
+    def both(y):
         top, bottom = y[:half], y[half:]
         return (
             jnp.where(low, top, roll(bottom, HALF)),
             jnp.where(low, roll(top, HALF), bottom),
         )
 
-    k, v = both(key_w, value_w)
+    k, v = both(full[:, :LANES])
     kv[:half, :] = k.astype(BF16)
     kv[half:, :] = v.astype(BF16)
-    q, g = both(query_w, gate_w)
+    q, g = both(full[:, LANES:])
     query[...] = q.astype(BF16)
     gate[...] = jax.nn.sigmoid(g)
 
@@ -436,16 +438,18 @@
         close_t[t] = jax.nn.sigmoid(dot_nn(w_close, norm_t[t]))
 
 
-def triangle_body(rows, part, left_pk, own, sib, across, across_sib, mine, other):
+def triangle_body(rows, left_pk, own, sib, across, across_sib, *outs):
+    mines, others = outs[: len(outs) // 2], outs[len(outs) // 2 :]
+    n = rows // len(mines)
     col = lax.axis_index("col")
     row = lax.axis_index("row")
     chip_y, core = row // 2, row % 2
     is_low, here = core == 0, chip_y == col
-    n = rows // 2
-    low = lane_of((n, LANES)) < HALF
-    for ch in range(left_pk.shape[0] // rows):
+    low = lane_of((rows, LANES)) < HALF
+
+    def product(ch):
         cut = slice(ch * rows, (ch + 1) * rows)
-        a = left_pk[ch * rows + part * n : ch * rows + (part + 1) * n, :]
+        a = left_pk[cut, :]
         zero = jnp.zeros_like(a)
         lhs = jnp.concatenate([jnp.where(low, a, zero), jnp.where(low, zero, a)], axis=0)
         o, s, x, xs = own[cut, :], sib[cut, :], across[cut, :], across_sib[cut, :]
@@ -459,51 +463,58 @@
             axis=0,
         )
         prod = dot_nt(lhs, rhs)
-        u, v = prod[:n], prod[n:]
-        to = slice(ch * n, (ch + 1) * n)
-        mine[to, :] = jnp.where(low, u, roll(v, HALF))
-        other[to, :] = jnp.where(low, roll(u, HALF), v).astype(BF16)
-
-
-def final_body(n, part, *refs):
-    half_own, half_far, mid_t, close_t, final_w, out_h, scr, out, *sems = refs[part:]
+        u, v = prod[:rows], prod[rows:]
+        return jnp.where(low, u, roll(v, HALF)), jnp.where(low, roll(u, HALF), v)
+
+    for ch in range(0, left_pk.shape[0] // rows, 2):
+        (m0, o0), (m1, o1) = product(ch), product(ch + 1)
+        to = slice(ch * n, (ch + 2) * n)
+        for part in range(len(mines)):
+            cut = slice(part * n, (part + 1) * n)
+            mines[part][to, :] = jnp.concatenate([m0[cut], m1[cut]], axis=0)
+            others[part][to, :] = jnp.concatenate([o0[cut], o1[cut]], axis=0).astype(BF16)
+
+
+def final_body(n, first, count, *refs):
+    refs = refs[1:] if first else refs
+    halves, refs = refs[: 2 * count], refs[2 * count :]
+    mid_t, close_t, final_w, out_h, scr, out, *sems = refs
     branch = lax.axis_index("branch")
-    chans = half_own.shape[0] // n
+    chans = halves[0].shape[0] // n
     low = lane_of((chans, LANES)) < HALF
-    for h, half in enumerate((half_own, half_far)):
-        for c in range(chans):
-            scr[h, c * (n + PAD) : c * (n + PAD) + n, :] = half[c * n : (c + 1) * n, :].astype(F32)
+    for k, half in enumerate(halves):
+        scr[k] = half[...].astype(F32)
     owners = [branch, branch ^ 2, branch ^ 1, branch ^ 3]
     w_t = [final_w[pl.ds(pl.multiple_of(o * chans, chans), chans), :] for o in owners]
     w_t = jnp.transpose(jnp.concatenate(w_t, axis=0).astype(F32)).astype(BF16)
-    tiles = n // 2
-    per = tiles // len(sems)
-    base = part * tiles
+    per = n // 2
+    base = first * per
     moves = []
 
-    def normed(t):
+    def normed(chunk, t):
         blocks = []
         for h in range(2):
-            z0 = scr[h, pl.ds(2 * t, chans, stride=n + PAD), :]
-            z1 = scr[h, pl.ds(2 * t + 1, chans, stride=n + PAD), :]
+            z0 = scr[2 * chunk + h, pl.ds(2 * t, chans, stride=n), :]
+            z1 = scr[2 * chunk + h, pl.ds(2 * t + 1, chans, stride=n), :]
             blocks += [jnp.where(low, z0, roll(z1, HALF)), jnp.where(low, roll(z0, HALF), z1)]
         x = jnp.concatenate(blocks, axis=0)
         x = x - jnp.mean(x, axis=0, keepdims=True)
         x = x * lax.rsqrt(jnp.mean(x * x, axis=0, keepdims=True) + EPS)
         return x.astype(BF16)
 
-    for start in range(0, tiles, per):
-        change = dot_nn(
-            w_t, jnp.concatenate([normed(t) for t in range(start, start + per)], axis=1)
-        )
-        for e in range(per):
-            t = start + e
-            part_of = change[:, e * LANES : (e + 1) * LANES]
-            result = mid_t[base + t].astype(F32) + close_t[base + t] * part_of
-            out[t * LANES : (t + 1) * LANES, :] = jnp.transpose(result.astype(BF16))
-        here = out.at[pl.ds(start * LANES, per * LANES)]
-        there = out_h.at[pl.ds((base + start) * LANES, per * LANES)]
-        moves.append(pltpu.make_async_copy(here, there, sems[start // per]))
+    for chunk in range(count):
+        for start in range(0, per, 2):
+            change = dot_nn(
+                w_t, jnp.concatenate([normed(chunk, start), normed(chunk, start + 1)], axis=1)
+            )
+            for e in range(2):
+                t = chunk * per + start + e
+                part_of = change[:, e * LANES : (e + 1) * LANES]
+                result = mid_t[base + t].astype(F32) + close_t[base + t] * part_of
+                out[t * LANES : (t + 1) * LANES, :] = jnp.transpose(result.astype(BF16))
+        here = out.at[pl.ds(chunk * per * LANES, per * LANES)]
+        there = out_h.at[pl.ds((base + chunk * per) * LANES, per * LANES)]
+        moves.append(pltpu.make_async_copy(here, there, sems[chunk]))
         moves[-1].start()
     for move in moves:
         move.wait()
@@ -717,14 +728,13 @@
     )(query, gate, kv, kv_s, kv_x, kv_xs, message, got, scoring_final_matrix)
     right_xs = send(right_x, other_core)
 
-    mines, fars = [], []
-    for part in range(2):
-        mine, other = call(
-            functools.partial(triangle_body, rows, part),
-            [((quarter * rows // 2, LANES), F32), ((quarter * rows // 2, LANES), BF16)],
-        )(left_pk, right_pk, right_s, right_x, right_xs)
-        mines.append(mine)
-        fars.append(send(other, other_col))
+    chunks = 4
+    piece = (quarter * rows // chunks, LANES)
+    products = call(
+        functools.partial(triangle_body, rows), [(piece, F32)] * chunks + [(piece, BF16)] * chunks
+    )(left_pk, right_pk, right_s, right_x, right_xs)
+    mines = products[:chunks]
+    fars = [send(x, other_col) for x in products[chunks:]]
     (close_t,) = call(close_body, [((tiles, chans, LANES), F32)])(norm_t, trio_sigmoid_matrix)
     parts = [parts[0]] + [send(parts[m], lambda b, r, c, m=m: (b ^ m, r, c)) for m in range(1, n_b)]
     half_own = [(mine + far.astype(F32)).astype(BF16) for mine, far in zip(mines, fars)]
@@ -732,17 +742,21 @@
     (revised,) = call(revise_body, [((n_rows, depth // n_b), BF16)])(hom, *parts)
 
     pair_out = ()
-    for part in range(2):
+    for first, count in ((0, chunks // 2), (chunks // 2, chunks - chunks // 2)):
+        ends = [x for k in range(first, first + count) for x in (half_own[k], half_far[k])]
         pair_out = call(
-            functools.partial(final_body, rows // 2, part),
+            functools.partial(final_body, rows // chunks, first, count),
             [((rows * block, chans), BF16)],
-            [((2, quarter * (rows // 2 + PAD), LANES), F32), ((rows * block // 2, chans), BF16)],
+            [
+                ((2 * count,) + piece, F32),
+                ((rows * block * count // chunks, chans), BF16),
+            ],
             mib=12,
-            sems=4,
+            sems=count,
             out_hbm=1,
-            anywhere=part,
-            alias={0: 0} if part else None,
-        )(*pair_out, half_own[part], half_far[part], mid_t, close_t, trio_final_matrix)
+            anywhere=min(first, 1),
+            alias={0: 0} if first else None,
+        )(*pair_out, *ends, mid_t, close_t, trio_final_matrix)
     (pair_out,) = pair_out
     return (
         revised.reshape(share, rows, depth // n_b),

time: 58.5 us -> 61 us (1.043)
  starting transfers between devices: 21 us -> 25.4 us
  waiting for transfers between devices: 23 us -> 21.7 us
    ppermute x18 -> x22, starting transfers between devices: 21 us -> 25.4 us  [send(): return lax.ppermute(x, AXES, pairs)]
    ppermute x18 -> x22, waiting for transfers between devices: 23 us -> 21.7 us  [send(): return lax.ppermute(x, AXES, pairs)]
    pallas_call x13 -> x12, Pallas kernels: 13.3 us -> 12.7 us  [run(): pl.pallas_call(body, out_shape=tuple((jax.ShapeDtypeStruct(s, d) for s, d...]
  transfers between devices with their start and end apart: 18 -> 22, of which waited for: 8 -> 9; matrix products, arithmetic and copies ran while one was open for 0% -> 0% of each run, Pallas kernels for 16% -> 15%
where the time goes in v2:
time: 61 us; the launch traced here: 60.8 us
  starting transfers between devices  25.4 us (42%)
  waiting for transfers between devices  21.7 us (36%)
  Pallas kernels  12.7 us (21%)
  between operations  0.87 us (1%)
    ppermute x22, starting transfers between devices, send(): return lax.ppermute(x, AXES, pairs)  25.4 us
    ppermute x22, waiting for transfers between devices, send(): return lax.ppermute(x, AXES, pairs)  21.7 us
    pallas_call x12, Pallas kernels, run(): pl.pallas_call(body, out_shape=tuple((jax.ShapeDtypeStruct(s, d) for s, d...  12.7 us
  transfers between devices with their start and end apart: 22, of which 9 were waited for; matrix products, arithmetic and copies ran while one was open for 0% of the time, Pallas kernels for 15%

profile of v2, /device:TPU:0, one launch (start us, length us, event | category | flops | bytes accessed | tf_op | source)
XLA Modules:
  0.0 60.8 jit_solution(12025038618371717430)
XLA Ops:
  0.6 2.2 %shard_map.158 = (bf16[1024,256]{1,0:T(8,128)(2,1)S(1)}, bf16[256,128]{1,0:T(8,128)(2,1)S(1)}, bf16[256,128]{1,0:T(8,128)(2,1)S(1)}, bf16[2048,128]{1,0:T(8,128)...) custom-call(bf16[1024,256]{1,0:T(8,128)(2,1)} %bitcast.13, ...), custom_call_target="tpu_custom_call" | custom-call | flops 1000000 | bytes 524288 | tf_op jit(solution)/shard_map/pallas_call | solution.py:217
  2.8 0.6 collective-permute-start.7
  3.4 0.9 %collective-permute-done.7.sib_r = bf16[256,128]{1,0:T(8,128)(2,1)S(1)} collective-permute-done((bf16[256,128]{1,0:T(8,128)(2,1)S(1)}, bf16[256,128]{1,0:T(8,128)(2,1)S(1)}, u32[]{:S(2)}, u32[]{:S(2)}) %collective-permute-start.7) | collective-permute-done | bytes 65568 | tf_op jit(solution)/shard_map/ppermute | solution.py:635
  4.3 4.8 %collective-permute-start.8 = (bf16[512,128]{1,0:T(8,128)(2,1)S(1)}, bf16[512,128]{1,0:T(8,128)(2,1)S(1)}, u32[]{:S(2)}, u32[]{:S(2)}) collective-permute-start(bf16[512,128]{1,0:T(8,128)(2,1)S(1)} %pad_maximum_fusion), channel_id=1, source_target_pairs={{1,0},{5,1},{6,3},{0,4},{4,5},{3,6},{9,8},{13,9},{14,11},{8,12},{1... | collective-permute-start | bytes 393224 | tf_op jit(solution)/shard_map/ppermute | solution.py:635
  9.1 3.9 %collective-permute-done.8.got = bf16[512,128]{1,0:T(8,128)(2,1)S(1)} collective-permute-done((bf16[512,128]{1,0:T(8,128)(2,1)S(1)}, bf16[512,128]{1,0:T(8,128)(2,1)S(1)}, u32[]{:S(2)}, u32[]{:S(2)}) %collective-permute-start.8) | collective-permute-done | bytes 131104 | tf_op jit(solution)/shard_map/ppermute | solution.py:635
  13.0 0.0 collective-permute-start.9
  13.0 0.6 shard_map.160
  13.6 2.5 %collective-permute-start.3 = (bf16[288,128]{1,0:T(8,128)(2,1)S(1)}, bf16[288,128]{1,0:T(8,128)(2,1)S(1)}, u32[]{:S(2)}, u32[]{:S(2)}) collective-permute-start(bf16[288,128]{1,0:T(8,128)(2,1)S(1)} %get-tuple-element.37.sent.left_own), channel_id=1, source_target_pairs={{1,0},{0,1},{3,2},{2,3},{5,4},{4,5},{7,6},{6,7},{9,8},{8,9},{11,10... | collective-permute-start | bytes 221192 | tf_op jit(solution)/shard_map/ppermute | solution.py:635
  16.0 2.6 %collective-permute-start.10 = (bf16[4,32,128]{2,1,0:T(8,128)(2,1)S(1)}, bf16[4,32,128]{2,1,0:T(8,128)(2,1)S(1)}, u32[]{:S(2)}, u32[]{:S(2)}) collective-permute-start(bf16[4,32,128]{2,1,0:T(8,128)(2,1)S(1)} %get-tuple-element.46.w_own), channel_id=1, source_target_pairs={{16,0},{17,1},{18,2},{19,3},{20,4},{21,5},{22,6},{23,7},{24,8},{25... | collective-permute-start | bytes 98312 | tf_op jit(solution)/shard_map/ppermute | solution.py:635
  18.6 0.3 collective-permute-done.3.got.left_far
  19.0 0.0 collective-permute-done.9.got_sib
  19.0 2.2 %shard_map.163 = (bf16[16,128,128]{2,1,0:T(8,128)(2,1)S(1)}, bf16[16,128,128]{2,1,0:T(8,128)(2,1)S(1)}) custom-call(bf16[16,128,128]{2,1,0:T(8,128)(2,1)S(1)} %get-tuple-element.42.couple_t, bf16[128,1024]{1,0:T(8,128)(2,1)S(1)} %get-tuple-element.43.outer_wt, bf16[288,128]{1,0:T(8,128)(2,1)S(1)} %get-tuple-element.37.sent.left_own, ...), custom_call_target="tpu_custom_call" | custom-call | flops 1000000 | bytes 524288 | tf_op jit(solution)/shard_map/pallas_call | solution.py:217
  21.2 0.0 collective-permute-done.10.w_far
  21.2 0.0 copy-start.2
  21.2 0.0 copy-start.3
  21.3 0.0 copy-start.4
  21.3 0.0 copy-start.5
  21.3 0.4 shard_map.165.own
  21.7 1.8 %collective-permute-start.12 = (bf16[1024,128]{1,0:T(8,128)(2,1)S(1)}, bf16[1024,128]{1,0:T(8,128)(2,1)S(1)}, u32[]{:S(2)}, u32[]{:S(2)}) collective-permute-start(bf16[1024,128]{1,0:T(8,128)(2,1)S(1)} %shard_map.165.own), channel_id=1, source_target_pairs={{4,0},{5,1},{6,2},{7,3},{0,4},{1,5},{2,6},{3,7},{12,8},{13,9},{14,... | collective-permute-start | bytes 786440 | tf_op jit(solution)/shard_map/ppermute | solution.py:635
  23.5 0.0 copy-done.3
  23.5 0.4 shard_map.159
  24.0 0.3 collective-permute-start.1
  24.3 0.0 collective-permute-start.11
  24.3 6.6 %collective-permute-done.12.across = bf16[1024,128]{1,0:T(8,128)(2,1)S(1)} collective-permute-done((bf16[1024,128]{1,0:T(8,128)(2,1)S(1)}, bf16[1024,128]{1,0:T(8,128)(2,1)S(1)}, u32[]{:S(2)}, u32[]{:S(2)}) %collective-permute-start.12) | collective-permute-done | bytes 262176 | tf_op jit(solution)/shard_map/ppermute | solution.py:635
  30.9 0.0 collective-permute-start.13
  30.9 0.5 collective-permute-start
  31.4 4.1 %collective-permute-done.1.across = bf16[1024,128]{1,0:T(8,128)(2,1)S(1)} collective-permute-done((bf16[1024,128]{1,0:T(8,128)(2,1)S(1)}, bf16[1024,128]{1,0:T(8,128)(2,1)S(1)}, u32[]{:S(2)}, u32[]{:S(2)}) %collective-permute-start.1) | collective-permute-done | bytes 262176 | tf_op jit(solution)/shard_map/ppermute | solution.py:635
  35.5 0.0 collective-permute-start.2
  35.5 0.4 shard_map.164.left_pk
  35.9 0.0 copy-start.6
  35.9 0.0 collective-permute-done.11.sib
  36.0 0.0 collective-permute-done.13.across_sib
  36.0 0.9 %shard_map.166 = (f32[256,128]{1,0:T(8,128)S(1)}, f32[256,128]{1,0:T(8,128)S(1)}, f32[256,128]{1,0:T(8,128)S(1)}, f32[256,128]{1,0:T(8,128)S(1)}, bf16[256,128]{...) custom-call(bf16[1024,128]{1,0:T(8,128)(2,1)S(1)} %shard_map.164.lef, ...), custom_call_target="tpu_custom_call" | custom-call | flops 1000000 | bytes 524288 | tf_op jit(solution)/shard_map/pallas_call | solution.py:217
  36.9 1.5 %collective-permute-start.14 = (bf16[256,128]{1,0:T(8,128)(2,1)S(1)}, bf16[256,128]{1,0:T(8,128)(2,1)S(1)}, u32[]{:S(2)}, u32[]{:S(2)}) collective-permute-start(bf16[256,128]{1,0:T(8,128)(2,1)S(1)} %get-tuple-element.48), channel_id=1, source_target_pairs={{1,0},{0,1},{3,2},{2,3},{5,4},{4,5},{7,6},{6,7},{9,8},{8,9},{11,10... | collective-permute-start | bytes 196616 | tf_op jit(solution)/shard_map/ppermute | solution.py:635
  38.4 0.0 collective-permute-done.sib
  38.4 0.0 collective-permute-done.2.across_sib
  38.4 1.7 %shard_map.161 = (bf16[512,128]{1,0:T(8,128)(2,1)S(1)}, bf16[512,128]{1,0:T(8,128)(2,1)S(1)}, bf16[512,128]{1,0:T(8,128)(2,1)S(1)}, bf16[512,128]{1,0:T(8,128)(2,1)S(1)}) custom-call(bf16[512,128]{1,0:T(8,128)(2,1)S(1)} %get-tuple-element.30.query, f32[512,128]{1,0:T(8,128)S(1)} %get-tuple-element.31.gate, bf16[1024,128]{1,0:T(8,128)(2,1)S(1)} %get-tuple-element.32.own, ...), custom_call_target="tpu_custom_call" | custom-call | flops 1000000 | bytes 524288 | tf_op jit(solution)/shard_map/pallas_call | solution.py:217
  40.2 1.6 %collective-permute-start.4 = (bf16[512,128]{1,0:T(8,128)(2,1)S(1)}, bf16[512,128]{1,0:T(8,128)(2,1)S(1)}, u32[]{:S(2)}, u32[]{:S(2)}) collective-permute-start(bf16[512,128]{1,0:T(8,128)(2,1)S(1)} %get-tuple-element.39), channel_id=1, source_target_pairs={{8,0},{9,1},{10,2},{11,3},{12,4},{13,5},{14,6},{15,7},{0,8},{1,9},... | collective-permute-start | bytes 393224 | tf_op jit(solution)/shard_map/ppermute | solution.py:635
  41.8 2.6 %collective-permute-start.5 = (bf16[512,128]{1,0:T(8,128)(2,1)S(1)}, bf16[512,128]{1,0:T(8,128)(2,1)S(1)}, u32[]{:S(2)}, u32[]{:S(2)}) collective-permute-start(bf16[512,128]{1,0:T(8,128)(2,1)S(1)} %get-tuple-element.40), channel_id=1, source_target_pairs={{16,0},{17,1},{18,2},{19,3},{20,4},{21,5},{22,6},{23,7},{24,8},{25... | collective-permute-start | bytes 393224 | tf_op jit(solution)/shard_map/ppermute | solution.py:635
  44.4 0.2 collective-permute-start.6
  44.6 0.6 collective-permute-start.16
  45.2 0.0 collective-permute-done.14
  45.2 1.5 %collective-permute-start.18 = (bf16[256,128]{1,0:T(8,128)(2,1)S(1)}, bf16[256,128]{1,0:T(8,128)(2,1)S(1)}, u32[]{:S(2)}, u32[]{:S(2)}) collective-permute-start(bf16[256,128]{1,0:T(8,128)(2,1)S(1)} %get-tuple-element.53), channel_id=1, source_target_pairs={{1,0},{0,1},{3,2},{2,3},{5,4},{4,5},{7,6},{6,7},{9,8},{8,9},{11,10... | collective-permute-start | bytes 196616 | tf_op jit(solution)/shard_map/ppermute | solution.py:635
  46.7 2.2 %collective-permute-done.16 = bf16[256,128]{1,0:T(8,128)(2,1)S(1)} collective-permute-done((bf16[256,128]{1,0:T(8,128)(2,1)S(1)}, bf16[256,128]{1,0:T(8,128)(2,1)S(1)}, u32[]{:S(2)}, u32[]{:S(2)}) %collective-permute-start.16) | collective-permute-done | bytes 65568 | tf_op jit(solution)/shard_map/ppermute | solution.py:635
  48.9 0.9 %collective-permute-start.20 = (bf16[256,128]{1,0:T(8,128)(2,1)S(1)}, bf16[256,128]{1,0:T(8,128)(2,1)S(1)}, u32[]{:S(2)}, u32[]{:S(2)}) collective-permute-start(bf16[256,128]{1,0:T(8,128)(2,1)S(1)} %get-tuple-element.55), channel_id=1, source_target_pairs={{1,0},{0,1},{3,2},{2,3},{5,4},{4,5},{7,6},{6,7},{9,8},{8,9},{11,10... | collective-permute-start | bytes 196616 | tf_op jit(solution)/shard_map/ppermute | solution.py:635
  49.8 0.0 collective-permute-done.18
  49.8 0.7 %collective-permute-start.15 = (bf16[256,128]{1,0:T(8,128)(2,1)S(1)}, bf16[256,128]{1,0:T(8,128)(2,1)S(1)}, u32[]{:S(2)}, u32[]{:S(2)}) collective-permute-start(bf16[256,128]{1,0:T(8,128)(2,1)S(1)} %add_convert_fusion.3.refs_0_), channel_id=1, source_target_pairs={{8,0},{9,1},{10,2},{11,3},{12,4},{13,5},{14,6},{15,7},{0,8},{1,9},... | collective-permute-start | bytes 196616 | tf_op jit(solution)/shard_map/ppermute | solution.py:635
  50.5 2.6 %collective-permute-done.20 = bf16[256,128]{1,0:T(8,128)(2,1)S(1)} collective-permute-done((bf16[256,128]{1,0:T(8,128)(2,1)S(1)}, bf16[256,128]{1,0:T(8,128)(2,1)S(1)}, u32[]{:S(2)}, u32[]{:S(2)}) %collective-permute-start.20) | collective-permute-done | bytes 65568 | tf_op jit(solution)/shard_map/ppermute | solution.py:635
  53.2 0.7 %collective-permute-start.17 = (bf16[256,128]{1,0:T(8,128)(2,1)S(1)}, bf16[256,128]{1,0:T(8,128)(2,1)S(1)}, u32[]{:S(2)}, u32[]{:S(2)}) collective-permute-start(bf16[256,128]{1,0:T(8,128)(2,1)S(1)} %add_convert_fusion.2.refs_2_), channel_id=1, source_target_pairs={{8,0},{9,1},{10,2},{11,3},{12,4},{13,5},{14,6},{15,7},{0,8},{1,9},... | collective-permute-start | bytes 196616 | tf_op jit(solution)/shard_map/ppermute | solution.py:635
  53.9 0.0 copy-start
  53.9 0.0 collective-permute-done.4.p1
  53.9 1.4 %collective-permute-start.19 = (bf16[256,128]{1,0:T(8,128)(2,1)S(1)}, bf16[256,128]{1,0:T(8,128)(2,1)S(1)}, u32[]{:S(2)}, u32[]{:S(2)}) collective-permute-start(bf16[256,128]{1,0:T(8,128)(2,1)S(1)} %add_convert_fusion.1.refs_1_), channel_id=1, source_target_pairs={{8,0},{9,1},{10,2},{11,3},{12,4},{13,5},{14,6},{15,7},{0,8},{1,9},... | collective-permute-start | bytes 196616 | tf_op jit(solution)/shard_map/ppermute | solution.py:635
  55.3 0.0 collective-permute-done.5.p2
  55.3 0.7 %collective-permute-start.21 = (bf16[256,128]{1,0:T(8,128)(2,1)S(1)}, bf16[256,128]{1,0:T(8,128)(2,1)S(1)}, u32[]{:S(2)}, u32[]{:S(2)}) collective-permute-start(bf16[256,128]{1,0:T(8,128)(2,1)S(1)} %add_convert_fusion.refs_3_), channel_id=1, source_target_pairs={{8,0},{9,1},{10,2},{11,3},{12,4},{13,5},{14,6},{15,7},{0,8},{1,9},... | collective-permute-start | bytes 196616 | tf_op jit(solution)/shard_map/ppermute | solution.py:635
  56.0 0.4 shard_map.167.refs_5_.refs_6_
  56.4 0.0 collective-permute-done.6.p3
  56.4 0.0 copy-start.1
  56.4 0.9 %shard_map.162 = bf16[1024,64]{1,0:T(8,128)(2,1)} custom-call(bf16[1024,256]{1,0:T(8,128)(2,1)S(1)} %bitcast.14, bf16[512,128]{1,0:T(8,128)(2,1)S(1)} %get-tuple-element.38.p0, bf16[512,128]{1,0:T(8,128)(2,1)S(1)} %collective-permute-done.4.p1, bf16[512,128]{1,0:T(8,128)(2,1)S(1)} %collective-permute-done.5.p2, bf16[512,128]{1,0:T(8,128)(2,1)S(1)} %collective-permute-done.6.p3), custom_call_target="tpu_custom_call" | custom-call | flops 1000000 | bytes 524288 | tf_op jit(solution)/shard_map/pallas_call | solution.py:217
  57.3 0.0 collective-permute-done.15.refs_1_
  57.3 0.6 %collective-permute-done.17.refs_3_ = bf16[256,128]{1,0:T(8,128)(2,1)S(1)} collective-permute-done((bf16[256,128]{1,0:T(8,128)(2,1)S(1)}, bf16[256,128]{1,0:T(8,128)(2,1)S(1)}, u32[]{:S(2)}, u32[]{:S(2)}) %collective-permute-start.17) | collective-permute-done | bytes 65568 | tf_op jit(solution)/shard_map/ppermute | solution.py:635
  58.0 1.2 %shard_map.168.refs_0_ = bf16[2048,128]{1,0:T(8,128)(2,1)} custom-call(bf16[256,128]{1,0:T(8,128)(2,1)S(1)} %add_convert_fusion.3.refs_0_, bf16[256,128]{1,0:T(8,128)(2,1)S(1)} %collective-permute-done.15.refs_1_, bf16[256,128]{1,0:T(8,128)(2,1)S(1)} %add_convert_fusion.2.refs_2_, bf16[256,128]{1,0:T(8,128)(2,1)S(1)} %collective-permute-done.17.refs_3_, ...), custom_call_target="tpu_custom_call" | custom-call | flops 1000000 | bytes 524288 | tf_op jit(solution)/shard_map/pallas_call | solution.py:217
  59.2 0.0 collective-permute-done.19.refs_2_
  59.2 0.3 collective-permute-done.21.refs_4_
  59.6 1.2 %shard_map.169 = bf16[2048,128]{1,0:T(8,128)(2,1)} custom-call(bf16[2048,128]{1,0:T(8,128)(2,1)} %shard_map.168.refs_0_, bf16[256,128]{1,0:T(8,128)(2,1)S(1)} %add_convert_fusion.1.refs_1_, bf16[256,128]{1,0:T(8,128)(2,1)S(1)} %collective-permute-done.19.refs_2_, bf16[256,128]{1,0:T(8,128)(2,1)S(1)} %add_convert_fusion.refs_3_, ...), custom_call_target="tpu_custom_call", output_to_operand_aliasing={{}: (0, {})} | custom-call | flops 1000000 | bytes 524288 | tf_op jit(solution)/shard_map/pallas_call | solution.py:217
  (13 shorter events, 0.1 us)
Async XLA Ops:
  2.8 1.5 %collective-permute-start.7 = (bf16[256,128]{1,0:T(8,128)(2,1)S(1)}, bf16[256,128]{1,0:T(8,128)(2,1)S(1)}, u32[]{:S(2)}, u32[]{:S(2)}) collective-permute-start(bf16[256,128]{1,0:T(8,128)(2,1)S(1)} %get-tuple-element.44.own_r), channel_id=1, source_target_pairs={{2,0},{3,1},{0,2},{1,3},{6,4},{7,5},{4,6},{5,7},{10,8},{11,9},{8,1... | collective-permute-start | bytes 196616 | tf_op jit(solution)/shard_map/ppermute | solution.py:635
  4.3 8.7 %collective-permute-start.8 = (bf16[512,128]{1,0:T(8,128)(2,1)S(1)}, bf16[512,128]{1,0:T(8,128)(2,1)S(1)}, u32[]{:S(2)}, u32[]{:S(2)}) collective-permute-start(bf16[512,128]{1,0:T(8,128)(2,1)S(1)} %pad_maximum_fusion), channel_id=1, source_target_pairs={{1,0},{5,1},{6,3},{0,4},{4,5},{3,6},{9,8},{13,9},{14,11},{8,12},{1... | collective-permute-start | bytes 393224 | tf_op jit(solution)/shard_map/ppermute | solution.py:635
  13.0 6.0 %collective-permute-start.9 = (bf16[512,128]{1,0:T(8,128)(2,1)S(1)}, bf16[512,128]{1,0:T(8,128)(2,1)S(1)}, u32[]{:S(2)}, u32[]{:S(2)}) collective-permute-start(bf16[512,128]{1,0:T(8,128)(2,1)S(1)} %collective-permute-done.8.got), channel_id=1, source_target_pairs={{2,0},{3,1},{0,2},{1,3},{6,4},{7,5},{4,6},{5,7},{10,8},{11,9},{8,1... | collective-permute-start | bytes 393224 | tf_op jit(solution)/shard_map/ppermute | solution.py:635
  13.6 5.4 %collective-permute-start.3 = (bf16[288,128]{1,0:T(8,128)(2,1)S(1)}, bf16[288,128]{1,0:T(8,128)(2,1)S(1)}, u32[]{:S(2)}, u32[]{:S(2)}) collective-permute-start(bf16[288,128]{1,0:T(8,128)(2,1)S(1)} %get-tuple-element.37.sent.left_own), channel_id=1, source_target_pairs={{1,0},{0,1},{3,2},{2,3},{5,4},{4,5},{7,6},{6,7},{9,8},{8,9},{11,10... | collective-permute-start | bytes 221192 | tf_op jit(solution)/shard_map/ppermute | solution.py:635
  16.0 5.2 %collective-permute-start.10 = (bf16[4,32,128]{2,1,0:T(8,128)(2,1)S(1)}, bf16[4,32,128]{2,1,0:T(8,128)(2,1)S(1)}, u32[]{:S(2)}, u32[]{:S(2)}) collective-permute-start(bf16[4,32,128]{2,1,0:T(8,128)(2,1)S(1)} %get-tuple-element.46.w_own), channel_id=1, source_target_pairs={{16,0},{17,1},{18,2},{19,3},{20,4},{21,5},{22,6},{23,7},{24,8},{25... | collective-permute-start | bytes 98312 | tf_op jit(solution)/shard_map/ppermute | solution.py:635
  21.2 2.3 %copy-start.2 = (bf16[256,64]{0,1:T(8,128)(2,1)S(1)}, bf16[256,64]{0,1:T(8,128)(2,1)}, u32[]{:S(2)}) copy-start(bf16[256,64]{0,1:T(8,128)(2,1)} %param.18) | copy-start | bytes 98308
  21.2 2.3 %copy-start.3 = (bf16[256,64]{0,1:T(8,128)(2,1)S(1)}, bf16[256,64]{0,1:T(8,128)(2,1)}, u32[]{:S(2)}) copy-start(bf16[256,64]{0,1:T(8,128)(2,1)} %param.19) | copy-start | bytes 98308
  21.3 2.3 %copy-start.4 = (bf16[256,64]{0,1:T(8,128)(2,1)S(1)}, bf16[256,64]{0,1:T(8,128)(2,1)}, u32[]{:S(2)}) copy-start(bf16[256,64]{0,1:T(8,128)(2,1)} %param.17) | copy-start | bytes 98308
  21.3 2.3 %copy-start.5 = (bf16[256,64]{0,1:T(8,128)(2,1)S(1)}, bf16[256,64]{0,1:T(8,128)(2,1)}, u32[]{:S(2)}) copy-start(bf16[256,64]{0,1:T(8,128)(2,1)} %param.20) | copy-start | bytes 98308
  21.7 9.2 %collective-permute-start.12 = (bf16[1024,128]{1,0:T(8,128)(2,1)S(1)}, bf16[1024,128]{1,0:T(8,128)(2,1)S(1)}, u32[]{:S(2)}, u32[]{:S(2)}) collective-permute-start(bf16[1024,128]{1,0:T(8,128)(2,1)S(1)} %shard_map.165.own), channel_id=1, source_target_pairs={{4,0},{5,1},{6,2},{7,3},{0,4},{1,5},{2,6},{3,7},{12,8},{13,9},{14,... | collective-permute-start | bytes 786440 | tf_op jit(solution)/shard_map/ppermute | solution.py:635
  24.0 11.5 %collective-permute-start.1 = (bf16[1024,128]{1,0:T(8,128)(2,1)S(1)}, bf16[1024,128]{1,0:T(8,128)(2,1)S(1)}, u32[]{:S(2)}, u32[]{:S(2)}) collective-permute-start(bf16[1024,128]{1,0:T(8,128)(2,1)S(1)} %get-tuple-element.32.own), channel_id=1, source_target_pairs={{4,0},{5,1},{6,2},{7,3},{0,4},{1,5},{2,6},{3,7},{12,8},{13,9},{14,... | collective-permute-start | bytes 786440 | tf_op jit(solution)/shard_map/ppermute | solution.py:635
  24.3 11.6 %collective-permute-start.11 = (bf16[1024,128]{1,0:T(8,128)(2,1)S(1)}, bf16[1024,128]{1,0:T(8,128)(2,1)S(1)}, u32[]{:S(2)}, u32[]{:S(2)}) collective-permute-start(bf16[1024,128]{1,0:T(8,128)(2,1)S(1)} %shard_map.165.own), channel_id=1, source_target_pairs={{2,0},{3,1},{0,2},{1,3},{6,4},{7,5},{4,6},{5,7},{10,8},{11,9},{8,1... | collective-permute-start | bytes 786440 | tf_op jit(solution)/shard_map/ppermute | solution.py:635
  30.9 5.0 %collective-permute-start.13 = (bf16[1024,128]{1,0:T(8,128)(2,1)S(1)}, bf16[1024,128]{1,0:T(8,128)(2,1)S(1)}, u32[]{:S(2)}, u32[]{:S(2)}) collective-permute-start(bf16[1024,128]{1,0:T(8,128)(2,1)S(1)} %collective-permute-done.12.across), channel_id=1, source_target_pairs={{2,0},{3,1},{0,2},{1,3},{6,4},{7,5},{4,6},{5,7},{10,8},{11,9},{8,1... | collective-permute-start | bytes 786440 | tf_op jit(solution)/shard_map/ppermute | solution.py:635
  30.9 7.5 %collective-permute-start = (bf16[1024,128]{1,0:T(8,128)(2,1)S(1)}, bf16[1024,128]{1,0:T(8,128)(2,1)S(1)}, u32[]{:S(2)}, u32[]{:S(2)}) collective-permute-start(bf16[1024,128]{1,0:T(8,128)(2,1)S(1)} %get-tuple-element.32.own), channel_id=1, source_target_pairs={{2,0},{3,1},{0,2},{1,3},{6,4},{7,5},{4,6},{5,7},{10,8},{11,9},{8,1... | collective-permute-start | bytes 786440 | tf_op jit(solution)/shard_map/ppermute | solution.py:635
  35.5 2.9 %collective-permute-start.2 = (bf16[1024,128]{1,0:T(8,128)(2,1)S(1)}, bf16[1024,128]{1,0:T(8,128)(2,1)S(1)}, u32[]{:S(2)}, u32[]{:S(2)}) collective-permute-start(bf16[1024,128]{1,0:T(8,128)(2,1)S(1)} %collective-permute-done.1.across), channel_id=1, source_target_pairs={{2,0},{3,1},{0,2},{1,3},{6,4},{7,5},{4,6},{5,7},{10,8},{11,9},{8,1... | collective-permute-start | bytes 786440 | tf_op jit(solution)/shard_map/ppermute | solution.py:635
  35.9 2.5 %copy-start.6 = (bf16[64,256]{1,0:T(8,128)(2,1)S(1)}, bf16[64,256]{1,0:T(8,128)(2,1)}, u32[]{:S(2)}) copy-start(bf16[64,256]{1,0:T(8,128)(2,1)} %w_out.1) | copy-start | bytes 98308
  36.9 8.3 %collective-permute-start.14 = (bf16[256,128]{1,0:T(8,128)(2,1)S(1)}, bf16[256,128]{1,0:T(8,128)(2,1)S(1)}, u32[]{:S(2)}, u32[]{:S(2)}) collective-permute-start(bf16[256,128]{1,0:T(8,128)(2,1)S(1)} %get-tuple-element.48), channel_id=1, source_target_pairs={{1,0},{0,1},{3,2},{2,3},{5,4},{4,5},{7,6},{6,7},{9,8},{8,9},{11,10... | collective-permute-start | bytes 196616 | tf_op jit(solution)/shard_map/ppermute | solution.py:635
  40.2 13.7 %collective-permute-start.4 = (bf16[512,128]{1,0:T(8,128)(2,1)S(1)}, bf16[512,128]{1,0:T(8,128)(2,1)S(1)}, u32[]{:S(2)}, u32[]{:S(2)}) collective-permute-start(bf16[512,128]{1,0:T(8,128)(2,1)S(1)} %get-tuple-element.39), channel_id=1, source_target_pairs={{8,0},{9,1},{10,2},{11,3},{12,4},{13,5},{14,6},{15,7},{0,8},{1,9},... | collective-permute-start | bytes 393224 | tf_op jit(solution)/shard_map/ppermute | solution.py:635
  41.8 13.5 %collective-permute-start.5 = (bf16[512,128]{1,0:T(8,128)(2,1)S(1)}, bf16[512,128]{1,0:T(8,128)(2,1)S(1)}, u32[]{:S(2)}, u32[]{:S(2)}) collective-permute-start(bf16[512,128]{1,0:T(8,128)(2,1)S(1)} %get-tuple-element.40), channel_id=1, source_target_pairs={{16,0},{17,1},{18,2},{19,3},{20,4},{21,5},{22,6},{23,7},{24,8},{25... | collective-permute-start | bytes 393224 | tf_op jit(solution)/shard_map/ppermute | solution.py:635
  44.4 12.0 %collective-permute-start.6 = (bf16[512,128]{1,0:T(8,128)(2,1)S(1)}, bf16[512,128]{1,0:T(8,128)(2,1)S(1)}, u32[]{:S(2)}, u32[]{:S(2)}) collective-permute-start(bf16[512,128]{1,0:T(8,128)(2,1)S(1)} %get-tuple-element.41), channel_id=1, source_target_pairs={{24,0},{25,1},{26,2},{27,3},{28,4},{29,5},{30,6},{31,7},{16,8},{17... | collective-permute-start | bytes 393224 | tf_op jit(solution)/shard_map/ppermute | solution.py:635
  44.6 4.3 %collective-permute-start.16 = (bf16[256,128]{1,0:T(8,128)(2,1)S(1)}, bf16[256,128]{1,0:T(8,128)(2,1)S(1)}, u32[]{:S(2)}, u32[]{:S(2)}) collective-permute-start(bf16[256,128]{1,0:T(8,128)(2,1)S(1)} %get-tuple-element.50), channel_id=1, source_target_pairs={{1,0},{0,1},{3,2},{2,3},{5,4},{4,5},{7,6},{6,7},{9,8},{8,9},{11,10... | collective-permute-start | bytes 196616 | tf_op jit(solution)/shard_map/ppermute | solution.py:635
  45.2 4.6 %collective-permute-start.18 = (bf16[256,128]{1,0:T(8,128)(2,1)S(1)}, bf16[256,128]{1,0:T(8,128)(2,1)S(1)}, u32[]{:S(2)}, u32[]{:S(2)}) collective-permute-start(bf16[256,128]{1,0:T(8,128)(2,1)S(1)} %get-tuple-element.53), channel_id=1, source_target_pairs={{1,0},{0,1},{3,2},{2,3},{5,4},{4,5},{7,6},{6,7},{9,8},{8,9},{11,10... | collective-permute-start | bytes 196616 | tf_op jit(solution)/shard_map/ppermute | solution.py:635
  48.9 4.3 %collective-permute-start.20 = (bf16[256,128]{1,0:T(8,128)(2,1)S(1)}, bf16[256,128]{1,0:T(8,128)(2,1)S(1)}, u32[]{:S(2)}, u32[]{:S(2)}) collective-permute-start(bf16[256,128]{1,0:T(8,128)(2,1)S(1)} %get-tuple-element.55), channel_id=1, source_target_pairs={{1,0},{0,1},{3,2},{2,3},{5,4},{4,5},{7,6},{6,7},{9,8},{8,9},{11,10... | collective-permute-start | bytes 196616 | tf_op jit(solution)/shard_map/ppermute | solution.py:635
  49.8 7.5 %collective-permute-start.15 = (bf16[256,128]{1,0:T(8,128)(2,1)S(1)}, bf16[256,128]{1,0:T(8,128)(2,1)S(1)}, u32[]{:S(2)}, u32[]{:S(2)}) collective-permute-start(bf16[256,128]{1,0:T(8,128)(2,1)S(1)} %add_convert_fusion.3.refs_0_), channel_id=1, source_target_pairs={{8,0},{9,1},{10,2},{11,3},{12,4},{13,5},{14,6},{15,7},{0,8},{1,9},... | collective-permute-start | bytes 196616 | tf_op jit(solution)/shard_map/ppermute | solution.py:635
  53.2 4.8 %collective-permute-start.17 = (bf16[256,128]{1,0:T(8,128)(2,1)S(1)}, bf16[256,128]{1,0:T(8,128)(2,1)S(1)}, u32[]{:S(2)}, u32[]{:S(2)}) collective-permute-start(bf16[256,128]{1,0:T(8,128)(2,1)S(1)} %add_convert_fusion.2.refs_2_), channel_id=1, source_target_pairs={{8,0},{9,1},{10,2},{11,3},{12,4},{13,5},{14,6},{15,7},{0,8},{1,9},... | collective-permute-start | bytes 196616 | tf_op jit(solution)/shard_map/ppermute | solution.py:635
  53.8 2.1 %copy-start.7 = (bf16[128,128]{1,0:T(8,128)(2,1)S(1)}, bf16[128,128]{1,0:T(8,128)(2,1)}, u32[]{:S(2)}) copy-start(bf16[128,128]{1,0:T(8,128)(2,1)} %close_w.1) | copy-start | bytes 98308
  53.9 2.5 %copy-start = (bf16[32,32,256]{2,1,0:T(8,128)(2,1)S(1)}, bf16[32,32,256]{2,1,0:T(8,128)(2,1)}, u32[]{:S(2)}) copy-start(bf16[32,32,256]{2,1,0:T(8,128)(2,1)} %param.15) | copy-start | bytes 1572868
  53.9 5.3 %collective-permute-start.19 = (bf16[256,128]{1,0:T(8,128)(2,1)S(1)}, bf16[256,128]{1,0:T(8,128)(2,1)S(1)}, u32[]{:S(2)}, u32[]{:S(2)}) collective-permute-start(bf16[256,128]{1,0:T(8,128)(2,1)S(1)} %add_convert_fusion.1.refs_1_), channel_id=1, source_target_pairs={{8,0},{9,1},{10,2},{11,3},{12,4},{13,5},{14,6},{15,7},{0,8},{1,9},... | collective-permute-start | bytes 196616 | tf_op jit(solution)/shard_map/ppermute | solution.py:635
  55.3 4.3 %collective-permute-start.21 = (bf16[256,128]{1,0:T(8,128)(2,1)S(1)}, bf16[256,128]{1,0:T(8,128)(2,1)S(1)}, u32[]{:S(2)}, u32[]{:S(2)}) collective-permute-start(bf16[256,128]{1,0:T(8,128)(2,1)S(1)} %add_convert_fusion.refs_3_), channel_id=1, source_target_pairs={{8,0},{9,1},{10,2},{11,3},{12,4},{13,5},{14,6},{15,7},{0,8},{1,9},... | collective-permute-start | bytes 196616 | tf_op jit(solution)/shard_map/ppermute | solution.py:635
  56.4 1.6 %copy-start.1 = (bf16[128,128]{1,0:T(8,128)(2,1)S(1)}, bf16[128,128]{1,0:T(8,128)(2,1)}, u32[]{:S(2)}) copy-start(bf16[128,128]{1,0:T(8,128)(2,1)} %refs_7_.1) | copy-start | bytes 98308

commit v3 on v1

--- a/solution.py
+++ b/solution.py
@@ -282,18 +282,20 @@
     x = normed[...]
     low = lane_of((half, LANES)) < HALF
 
-    def both(w0, w1):
-        y = dot_nt(x, jnp.concatenate([w0[...], w1[...]], axis=0))
+    weights = [w[...] for w in (key_w, value_w, query_w, gate_w)]
+    full = dot_nt(x, jnp.concatenate(weights, axis=0))
+
+    def both(y):
         top, bottom = y[:half], y[half:]
         return (
             jnp.where(low, top, roll(bottom, HALF)),
             jnp.where(low, roll(top, HALF), bottom),
         )
 
-    k, v = both(key_w, value_w)
+    k, v = both(full[:, :LANES])
     kv[:half, :] = k.astype(BF16)
     kv[half:, :] = v.astype(BF16)
-    q, g = both(query_w, gate_w)
+    q, g = both(full[:, LANES:])
     query[...] = q.astype(BF16)
     gate[...] = jax.nn.sigmoid(g)
 

time: 58.5 us -> 58.5 us (level)
  no operation moved by 1% of the time
where the time goes in v3:
time: 58.5 us; the launch traced here: 58.2 us
  waiting for transfers between devices  23.1 us (39%)
  starting transfers between devices  21 us (36%)
  Pallas kernels  13.2 us (23%)
  between operations  0.82 us (1%)
    ppermute x18, waiting for transfers between devices, send(): return lax.ppermute(x, AXES, pairs)  23.1 us
    ppermute x18, starting transfers between devices, send(): return lax.ppermute(x, AXES, pairs)  21 us
    pallas_call x13, Pallas kernels, run(): pl.pallas_call(body, out_shape=tuple((jax.ShapeDtypeStruct(s, d) for s, d...  13.2 us
  transfers between devices with their start and end apart: 18, of which 8 were waited for; matrix products, arithmetic and copies ran while one was open for 0% of the time, Pallas kernels for 16%

profile of v3, /device:TPU:0, one launch (start us, length us, event | category | flops | bytes accessed | tf_op | source)
XLA Modules:
  0.0 58.2 jit_solution(1978003695105460305)
XLA Ops:
  0.6 2.2 %shard_map.158 = (bf16[1024,256]{1,0:T(8,128)(2,1)S(1)}, bf16[256,128]{1,0:T(8,128)(2,1)S(1)}, bf16[256,128]{1,0:T(8,128)(2,1)S(1)}, bf16[2048,128]{1,0:T(8,128)...) custom-call(bf16[1024,256]{1,0:T(8,128)(2,1)} %bitcast.13, ...), custom_call_target="tpu_custom_call" | custom-call | flops 1000000 | bytes 524288 | tf_op jit(solution)/shard_map/pallas_call | solution.py:217
  2.8 0.6 collective-permute-start.7
  3.4 0.9 %collective-permute-done.7.sib_r = bf16[256,128]{1,0:T(8,128)(2,1)S(1)} collective-permute-done((bf16[256,128]{1,0:T(8,128)(2,1)S(1)}, bf16[256,128]{1,0:T(8,128)(2,1)S(1)}, u32[]{:S(2)}, u32[]{:S(2)}) %collective-permute-start.7) | collective-permute-done | bytes 65568 | tf_op jit(solution)/shard_map/ppermute | solution.py:626
  4.3 4.8 %collective-permute-start.8 = (bf16[512,128]{1,0:T(8,128)(2,1)S(1)}, bf16[512,128]{1,0:T(8,128)(2,1)S(1)}, u32[]{:S(2)}, u32[]{:S(2)}) collective-permute-start(bf16[512,128]{1,0:T(8,128)(2,1)S(1)} %pad_maximum_fusion), channel_id=1, source_target_pairs={{1,0},{5,1},{6,3},{0,4},{4,5},{3,6},{9,8},{13,9},{14,11},{8,12},{1... | collective-permute-start | bytes 393224 | tf_op jit(solution)/shard_map/ppermute | solution.py:626
  9.1 3.9 %collective-permute-done.8.got = bf16[512,128]{1,0:T(8,128)(2,1)S(1)} collective-permute-done((bf16[512,128]{1,0:T(8,128)(2,1)S(1)}, bf16[512,128]{1,0:T(8,128)(2,1)S(1)}, u32[]{:S(2)}, u32[]{:S(2)}) %collective-permute-start.8) | collective-permute-done | bytes 131104 | tf_op jit(solution)/shard_map/ppermute | solution.py:626
  13.0 0.0 collective-permute-start.9
  13.0 0.6 %shard_map.160 = (bf16[16,128,128]{2,1,0:T(8,128)(2,1)S(1)}, bf16[288,128]{1,0:T(8,128)(2,1)S(1)}, bf16[128,1024]{1,0:T(8,128)(2,1)S(1)}) custom-call(bf16[2048,128]{1,0:T(8,128)(2,1)S(1)} %get-tuple-element.29.couple, bf16[2,128]{1,0:T(2,128)(2,1)S(1)} %get-tuple-element.30.offset_t, bf16[1024,128]{1,0:T(8,128)(2,1)S(1)} %get-tuple-element.31.outer_w, ...), custom_call_target="tpu_custom_call" | custom-call | flops 1000000 | bytes 524288 | tf_op jit(solution)/shard_map/pallas_call | solution.py:217
  13.6 2.5 %collective-permute-start.3 = (bf16[288,128]{1,0:T(8,128)(2,1)S(1)}, bf16[288,128]{1,0:T(8,128)(2,1)S(1)}, u32[]{:S(2)}, u32[]{:S(2)}) collective-permute-start(bf16[288,128]{1,0:T(8,128)(2,1)S(1)} %get-tuple-element.33.sent.left_own), channel_id=1, source_target_pairs={{1,0},{0,1},{3,2},{2,3},{5,4},{4,5},{7,6},{6,7},{9,8},{8,9},{11,10... | collective-permute-start | bytes 221192 | tf_op jit(solution)/shard_map/ppermute | solution.py:626
  16.0 2.6 %collective-permute-start.10 = (bf16[4,32,128]{2,1,0:T(8,128)(2,1)S(1)}, bf16[4,32,128]{2,1,0:T(8,128)(2,1)S(1)}, u32[]{:S(2)}, u32[]{:S(2)}) collective-permute-start(bf16[4,32,128]{2,1,0:T(8,128)(2,1)S(1)} %get-tuple-element.42.w_own), channel_id=1, source_target_pairs={{16,0},{17,1},{18,2},{19,3},{20,4},{21,5},{22,6},{23,7},{24,8},{25... | collective-permute-start | bytes 98312 | tf_op jit(solution)/shard_map/ppermute | solution.py:626
  18.6 0.3 collective-permute-done.3.got.left_far
  19.0 0.0 collective-permute-done.9.got_sib
  19.0 2.2 %shard_map.163 = (bf16[16,128,128]{2,1,0:T(8,128)(2,1)S(1)}, bf16[16,128,128]{2,1,0:T(8,128)(2,1)S(1)}) custom-call(bf16[16,128,128]{2,1,0:T(8,128)(2,1)S(1)} %get-tuple-element.38.couple_t, bf16[128,1024]{1,0:T(8,128)(2,1)S(1)} %get-tuple-element.39.outer_wt, bf16[288,128]{1,0:T(8,128)(2,1)S(1)} %get-tuple-element.33.sent.left_own, ...), custom_call_target="tpu_custom_call" | custom-call | flops 1000000 | bytes 524288 | tf_op jit(solution)/shard_map/pallas_call | solution.py:217
  21.2 0.0 collective-permute-done.10.w_far
  21.2 0.0 copy-start.2
  21.2 0.0 copy-start.3
  21.3 0.0 copy-start.4
  21.3 0.0 copy-start.5
  21.3 0.4 shard_map.165.own
  21.7 1.8 %collective-permute-start.12 = (bf16[1024,128]{1,0:T(8,128)(2,1)S(1)}, bf16[1024,128]{1,0:T(8,128)(2,1)S(1)}, u32[]{:S(2)}, u32[]{:S(2)}) collective-permute-start(bf16[1024,128]{1,0:T(8,128)(2,1)S(1)} %shard_map.165.own), channel_id=1, source_target_pairs={{4,0},{5,1},{6,2},{7,3},{0,4},{1,5},{2,6},{3,7},{12,8},{13,9},{14,... | collective-permute-start | bytes 786440 | tf_op jit(solution)/shard_map/ppermute | solution.py:626
  23.5 0.0 copy-done.2
  23.5 0.0 copy-done.3
  23.5 0.0 copy-done.4
  23.5 0.0 copy-done.5
  23.5 0.4 shard_map.159
  24.0 0.3 collective-permute-start.1
  24.3 0.0 collective-permute-start.11
  24.3 6.6 %collective-permute-done.12.across = bf16[1024,128]{1,0:T(8,128)(2,1)S(1)} collective-permute-done((bf16[1024,128]{1,0:T(8,128)(2,1)S(1)}, bf16[1024,128]{1,0:T(8,128)(2,1)S(1)}, u32[]{:S(2)}, u32[]{:S(2)}) %collective-permute-start.12) | collective-permute-done | bytes 262176 | tf_op jit(solution)/shard_map/ppermute | solution.py:626
  30.9 0.0 collective-permute-start.13
  30.9 0.5 collective-permute-start
  31.4 4.1 %collective-permute-done.1.across = bf16[1024,128]{1,0:T(8,128)(2,1)S(1)} collective-permute-done((bf16[1024,128]{1,0:T(8,128)(2,1)S(1)}, bf16[1024,128]{1,0:T(8,128)(2,1)S(1)}, u32[]{:S(2)}, u32[]{:S(2)}) %collective-permute-start.1) | collective-permute-done | bytes 262176 | tf_op jit(solution)/shard_map/ppermute | solution.py:626
  35.5 0.0 collective-permute-start.2
  35.5 0.4 shard_map.164.left_pk
  35.9 0.0 copy-start.6
  35.9 0.0 collective-permute-done.11.sib
  36.0 0.0 collective-permute-done.13.across_sib
  36.0 0.8 %shard_map.166 = (f32[512,128]{1,0:T(8,128)S(1)}, bf16[512,128]{1,0:T(8,128)(2,1)S(1)}) custom-call(bf16[1024,128]{1,0:T(8,128)(2,1)S(1)} %shard_map.164.left_pk, bf16[1024,128]{1,0:T(8,128)(2,1)S(1)} %shard_map.165.own, bf16[1024,128]{1,0:T(8,128)(2,1)S(1)} %collective-permute-done.11.sib, bf16[1024,128]{1,0:T(8,128)(2,1)S(1)} %collective-permute-done.12.across, ...), custom_call_target="tpu_custom_call" | custom-call | flops 1000000 | bytes 524288 | tf_op jit(solution)/shard_map/pallas_call | solution.py:217
  36.7 1.5 %collective-permute-start.14 = (bf16[512,128]{1,0:T(8,128)(2,1)S(1)}, bf16[512,128]{1,0:T(8,128)(2,1)S(1)}, u32[]{:S(2)}, u32[]{:S(2)}) collective-permute-start(bf16[512,128]{1,0:T(8,128)(2,1)S(1)} %get-tuple-element.44), channel_id=1, source_target_pairs={{1,0},{0,1},{3,2},{2,3},{5,4},{4,5},{7,6},{6,7},{9,8},{8,9},{11,10... | collective-permute-start | bytes 393224 | tf_op jit(solution)/shard_map/ppermute | solution.py:626
  38.2 0.0 collective-permute-done.sib
  38.2 0.0 collective-permute-done.2.across_sib
  38.2 0.0 copy-done.6
  38.3 1.7 %shard_map.161 = (bf16[512,128]{1,0:T(8,128)(2,1)S(1)}, bf16[512,128]{1,0:T(8,128)(2,1)S(1)}, bf16[512,128]{1,0:T(8,128)(2,1)S(1)}, bf16[512,128]{1,0:T(8,128)(2,1)S(1)}) custom-call(bf16[512,128]{1,0:T(8,128)(2,1)S(1)} %get-tuple-element.26.query, f32[512,128]{1,0:T(8,128)S(1)} %get-tuple-element.27.gate, bf16[1024,128]{1,0:T(8,128)(2,1)S(1)} %get-tuple-element.28.own, ...), custom_call_target="tpu_custom_call" | custom-call | flops 1000000 | bytes 524288 | tf_op jit(solution)/shard_map/pallas_call | solution.py:217
  40.0 1.6 %collective-permute-start.4 = (bf16[512,128]{1,0:T(8,128)(2,1)S(1)}, bf16[512,128]{1,0:T(8,128)(2,1)S(1)}, u32[]{:S(2)}, u32[]{:S(2)}) collective-permute-start(bf16[512,128]{1,0:T(8,128)(2,1)S(1)} %get-tuple-element.35), channel_id=1, source_target_pairs={{8,0},{9,1},{10,2},{11,3},{12,4},{13,5},{14,6},{15,7},{0,8},{1,9},... | collective-permute-start | bytes 393224 | tf_op jit(solution)/shard_map/ppermute | solution.py:626
  41.6 2.6 %collective-permute-start.5 = (bf16[512,128]{1,0:T(8,128)(2,1)S(1)}, bf16[512,128]{1,0:T(8,128)(2,1)S(1)}, u32[]{:S(2)}, u32[]{:S(2)}) collective-permute-start(bf16[512,128]{1,0:T(8,128)(2,1)S(1)} %get-tuple-element.36), channel_id=1, source_target_pairs={{16,0},{17,1},{18,2},{19,3},{20,4},{21,5},{22,6},{23,7},{24,8},{25... | collective-permute-start | bytes 393224 | tf_op jit(solution)/shard_map/ppermute | solution.py:626
  44.2 0.2 collective-permute-start.6
  44.4 0.7 %shard_map.169 = (f32[512,128]{1,0:T(8,128)S(1)}, bf16[512,128]{1,0:T(8,128)(2,1)S(1)}) custom-call(bf16[1024,128]{1,0:T(8,128)(2,1)S(1)} %shard_map.164.left_pk, bf16[1024,128]{1,0:T(8,128)(2,1)S(1)} %shard_map.165.own, bf16[1024,128]{1,0:T(8,128)(2,1)S(1)} %collective-permute-done.11.sib, bf16[1024,128]{1,0:T(8,128)(2,1)S(1)} %collective-permute-done.12.across, ...), custom_call_target="tpu_custom_call" | custom-call | flops 1000000 | bytes 524288 | tf_op jit(solution)/shard_map/pallas_call | solution.py:217
  45.2 0.6 %collective-permute-start.16 = (bf16[512,128]{1,0:T(8,128)(2,1)S(1)}, bf16[512,128]{1,0:T(8,128)(2,1)S(1)}, u32[]{:S(2)}, u32[]{:S(2)}) collective-permute-start(bf16[512,128]{1,0:T(8,128)(2,1)S(1)} %get-tuple-element.47), channel_id=1, source_target_pairs={{1,0},{0,1},{3,2},{2,3},{5,4},{4,5},{7,6},{6,7},{9,8},{8,9},{11,10... | collective-permute-start | bytes 393224 | tf_op jit(solution)/shard_map/ppermute | solution.py:626
  45.8 0.0 collective-permute-done.14
  45.8 0.6 collective-permute-start.15
  46.4 3.8 %collective-permute-done.16 = bf16[512,128]{1,0:T(8,128)(2,1)S(1)} collective-permute-done((bf16[512,128]{1,0:T(8,128)(2,1)S(1)}, bf16[512,128]{1,0:T(8,128)(2,1)S(1)}, u32[]{:S(2)}, u32[]{:S(2)}) %collective-permute-start.16) | collective-permute-done | bytes 131104 | tf_op jit(solution)/shard_map/ppermute | solution.py:626
  50.2 0.0 copy-start.7
  50.2 0.0 copy-start
  50.3 0.7 %collective-permute-start.17 = (bf16[512,128]{1,0:T(8,128)(2,1)S(1)}, bf16[512,128]{1,0:T(8,128)(2,1)S(1)}, u32[]{:S(2)}, u32[]{:S(2)}) collective-permute-start(bf16[512,128]{1,0:T(8,128)(2,1)S(1)} %add_convert_fusion.refs_1_), channel_id=1, source_target_pairs={{8,0},{9,1},{10,2},{11,3},{12,4},{13,5},{14,6},{15,7},{0,8},{1,9},... | collective-permute-start | bytes 393224 | tf_op jit(solution)/shard_map/ppermute | solution.py:626
  51.0 0.0 copy-done.7
  51.0 0.4 shard_map.167.refs_3_.refs_4_
  51.4 0.0 collective-permute-done.4.p1
  51.4 3.1 %collective-permute-done.5.p2 = bf16[512,128]{1,0:T(8,128)(2,1)S(1)} collective-permute-done((bf16[512,128]{1,0:T(8,128)(2,1)S(1)}, bf16[512,128]{1,0:T(8,128)(2,1)S(1)}, u32[]{:S(2)}, u32[]{:S(2)}) %collective-permute-start.5) | collective-permute-done | bytes 131104 | tf_op jit(solution)/shard_map/ppermute | solution.py:626
  54.5 0.0 collective-permute-done.6.p3
  54.5 0.0 copy-done
  54.5 0.9 %shard_map.162 = bf16[1024,64]{1,0:T(8,128)(2,1)} custom-call(bf16[1024,256]{1,0:T(8,128)(2,1)S(1)} %bitcast.14, bf16[512,128]{1,0:T(8,128)(2,1)S(1)} %get-tuple-element.34.p0, bf16[512,128]{1,0:T(8,128)(2,1)S(1)} %collective-permute-done.4.p1, bf16[512,128]{1,0:T(8,128)(2,1)S(1)} %collective-permute-done.5.p2, bf16[512,128]{1,0:T(8,128)(2,1)S(1)} %collective-permute-done.6.p3), custom_call_target="tpu_custom_call" | custom-call | flops 1000000 | bytes 524288 | tf_op jit(solution)/shard_map/pallas_call | solution.py:217
  55.5 0.0 collective-permute-done.15.refs_1_
  55.5 0.0 copy-done.1
  55.5 1.2 %shard_map.168.refs_0_ = bf16[2048,128]{1,0:T(8,128)(2,1)} custom-call(bf16[512,128]{1,0:T(8,128)(2,1)S(1)} %add_convert_fusion.1.refs_0_, bf16[512,128]{1,0:T(8,128)(2,1)S(1)} %collective-permute-done.15.refs_1_, bf16[16,128,128]{2,1,0:T(8,128)(2,1)S(1)} %get-tuple-element.45.refs_2_.refs_3_, f32[16,128,128]{2,1,0:T(8,128)S(1)} %shard_map.167.refs_3_.refs_4_, ...), custom_call_target="tpu_custom_call" | custom-call | flops 1000000 | bytes 524288 | tf_op jit(solution)/shard_map/pallas_call | solution.py:217
  56.7 0.3 collective-permute-done.17.refs_2_
  57.0 1.2 %shard_map.170 = bf16[2048,128]{1,0:T(8,128)(2,1)} custom-call(bf16[2048,128]{1,0:T(8,128)(2,1)} %shard_map.168.refs_0_, bf16[512,128]{1,0:T(8,128)(2,1)S(1)} %add_convert_fusion.refs_1_, bf16[512,128]{1,0:T(8,128)(2,1)S(1)} %collective-permute-done.17.refs_2_, ...), custom_call_target="tpu_custom_call", output_to_operand_aliasing={{}: (0, {})} | custom-call | flops 1000000 | bytes 524288 | tf_op jit(solution)/shard_map/pallas_call | solution.py:217
  (4 shorter events, 0.1 us)
Async XLA Ops:
  2.8 1.5 %collective-permute-start.7 = (bf16[256,128]{1,0:T(8,128)(2,1)S(1)}, bf16[256,128]{1,0:T(8,128)(2,1)S(1)}, u32[]{:S(2)}, u32[]{:S(2)}) collective-permute-start(bf16[256,128]{1,0:T(8,128)(2,1)S(1)} %get-tuple-element.40.own_r), channel_id=1, source_target_pairs={{2,0},{3,1},{0,2},{1,3},{6,4},{7,5},{4,6},{5,7},{10,8},{11,9},{8,1... | collective-permute-start | bytes 196616 | tf_op jit(solution)/shard_map/ppermute | solution.py:626
  4.3 8.7 %collective-permute-start.8 = (bf16[512,128]{1,0:T(8,128)(2,1)S(1)}, bf16[512,128]{1,0:T(8,128)(2,1)S(1)}, u32[]{:S(2)}, u32[]{:S(2)}) collective-permute-start(bf16[512,128]{1,0:T(8,128)(2,1)S(1)} %pad_maximum_fusion), channel_id=1, source_target_pairs={{1,0},{5,1},{6,3},{0,4},{4,5},{3,6},{9,8},{13,9},{14,11},{8,12},{1... | collective-permute-start | bytes 393224 | tf_op jit(solution)/shard_map/ppermute | solution.py:626
  13.0 6.0 %collective-permute-start.9 = (bf16[512,128]{1,0:T(8,128)(2,1)S(1)}, bf16[512,128]{1,0:T(8,128)(2,1)S(1)}, u32[]{:S(2)}, u32[]{:S(2)}) collective-permute-start(bf16[512,128]{1,0:T(8,128)(2,1)S(1)} %collective-permute-done.8.got), channel_id=1, source_target_pairs={{2,0},{3,1},{0,2},{1,3},{6,4},{7,5},{4,6},{5,7},{10,8},{11,9},{8,1... | collective-permute-start | bytes 393224 | tf_op jit(solution)/shard_map/ppermute | solution.py:626
  13.6 5.4 %collective-permute-start.3 = (bf16[288,128]{1,0:T(8,128)(2,1)S(1)}, bf16[288,128]{1,0:T(8,128)(2,1)S(1)}, u32[]{:S(2)}, u32[]{:S(2)}) collective-permute-start(bf16[288,128]{1,0:T(8,128)(2,1)S(1)} %get-tuple-element.33.sent.left_own), channel_id=1, source_target_pairs={{1,0},{0,1},{3,2},{2,3},{5,4},{4,5},{7,6},{6,7},{9,8},{8,9},{11,10... | collective-permute-start | bytes 221192 | tf_op jit(solution)/shard_map/ppermute | solution.py:626
  16.0 5.2 %collective-permute-start.10 = (bf16[4,32,128]{2,1,0:T(8,128)(2,1)S(1)}, bf16[4,32,128]{2,1,0:T(8,128)(2,1)S(1)}, u32[]{:S(2)}, u32[]{:S(2)}) collective-permute-start(bf16[4,32,128]{2,1,0:T(8,128)(2,1)S(1)} %get-tuple-element.42.w_own), channel_id=1, source_target_pairs={{16,0},{17,1},{18,2},{19,3},{20,4},{21,5},{22,6},{23,7},{24,8},{25... | collective-permute-start | bytes 98312 | tf_op jit(solution)/shard_map/ppermute | solution.py:626
  21.2 2.3 %copy-start.2 = (bf16[256,64]{0,1:T(8,128)(2,1)S(1)}, bf16[256,64]{0,1:T(8,128)(2,1)}, u32[]{:S(2)}) copy-start(bf16[256,64]{0,1:T(8,128)(2,1)} %param.18) | copy-start | bytes 98308
  21.2 2.3 %copy-start.3 = (bf16[256,64]{0,1:T(8,128)(2,1)S(1)}, bf16[256,64]{0,1:T(8,128)(2,1)}, u32[]{:S(2)}) copy-start(bf16[256,64]{0,1:T(8,128)(2,1)} %param.19) | copy-start | bytes 98308
  21.3 2.3 %copy-start.4 = (bf16[256,64]{0,1:T(8,128)(2,1)S(1)}, bf16[256,64]{0,1:T(8,128)(2,1)}, u32[]{:S(2)}) copy-start(bf16[256,64]{0,1:T(8,128)(2,1)} %param.17) | copy-start | bytes 98308
  21.3 2.3 %copy-start.5 = (bf16[256,64]{0,1:T(8,128)(2,1)S(1)}, bf16[256,64]{0,1:T(8,128)(2,1)}, u32[]{:S(2)}) copy-start(bf16[256,64]{0,1:T(8,128)(2,1)} %param.20) | copy-start | bytes 98308
  21.7 9.2 %collective-permute-start.12 = (bf16[1024,128]{1,0:T(8,128)(2,1)S(1)}, bf16[1024,128]{1,0:T(8,128)(2,1)S(1)}, u32[]{:S(2)}, u32[]{:S(2)}) collective-permute-start(bf16[1024,128]{1,0:T(8,128)(2,1)S(1)} %shard_map.165.own), channel_id=1, source_target_pairs={{4,0},{5,1},{6,2},{7,3},{0,4},{1,5},{2,6},{3,7},{12,8},{13,9},{14,... | collective-permute-start | bytes 786440 | tf_op jit(solution)/shard_map/ppermute | solution.py:626
  24.0 11.5 %collective-permute-start.1 = (bf16[1024,128]{1,0:T(8,128)(2,1)S(1)}, bf16[1024,128]{1,0:T(8,128)(2,1)S(1)}, u32[]{:S(2)}, u32[]{:S(2)}) collective-permute-start(bf16[1024,128]{1,0:T(8,128)(2,1)S(1)} %get-tuple-element.28.own), channel_id=1, source_target_pairs={{4,0},{5,1},{6,2},{7,3},{0,4},{1,5},{2,6},{3,7},{12,8},{13,9},{14,... | collective-permute-start | bytes 786440 | tf_op jit(solution)/shard_map/ppermute | solution.py:626
  24.3 11.6 %collective-permute-start.11 = (bf16[1024,128]{1,0:T(8,128)(2,1)S(1)}, bf16[1024,128]{1,0:T(8,128)(2,1)S(1)}, u32[]{:S(2)}, u32[]{:S(2)}) collective-permute-start(bf16[1024,128]{1,0:T(8,128)(2,1)S(1)} %shard_map.165.own), channel_id=1, source_target_pairs={{2,0},{3,1},{0,2},{1,3},{6,4},{7,5},{4,6},{5,7},{10,8},{11,9},{8,1... | collective-permute-start | bytes 786440 | tf_op jit(solution)/shard_map/ppermute | solution.py:626
  30.9 5.0 %collective-permute-start.13 = (bf16[1024,128]{1,0:T(8,128)(2,1)S(1)}, bf16[1024,128]{1,0:T(8,128)(2,1)S(1)}, u32[]{:S(2)}, u32[]{:S(2)}) collective-permute-start(bf16[1024,128]{1,0:T(8,128)(2,1)S(1)} %collective-permute-done.12.across), channel_id=1, source_target_pairs={{2,0},{3,1},{0,2},{1,3},{6,4},{7,5},{4,6},{5,7},{10,8},{11,9},{8,1... | collective-permute-start | bytes 786440 | tf_op jit(solution)/shard_map/ppermute | solution.py:626
  30.9 7.3 %collective-permute-start = (bf16[1024,128]{1,0:T(8,128)(2,1)S(1)}, bf16[1024,128]{1,0:T(8,128)(2,1)S(1)}, u32[]{:S(2)}, u32[]{:S(2)}) collective-permute-start(bf16[1024,128]{1,0:T(8,128)(2,1)S(1)} %get-tuple-element.28.own), channel_id=1, source_target_pairs={{2,0},{3,1},{0,2},{1,3},{6,4},{7,5},{4,6},{5,7},{10,8},{11,9},{8,1... | collective-permute-start | bytes 786440 | tf_op jit(solution)/shard_map/ppermute | solution.py:626
  35.5 2.7 %collective-permute-start.2 = (bf16[1024,128]{1,0:T(8,128)(2,1)S(1)}, bf16[1024,128]{1,0:T(8,128)(2,1)S(1)}, u32[]{:S(2)}, u32[]{:S(2)}) collective-permute-start(bf16[1024,128]{1,0:T(8,128)(2,1)S(1)} %collective-permute-done.1.across), channel_id=1, source_target_pairs={{2,0},{3,1},{0,2},{1,3},{6,4},{7,5},{4,6},{5,7},{10,8},{11,9},{8,1... | collective-permute-start | bytes 786440 | tf_op jit(solution)/shard_map/ppermute | solution.py:626
  35.9 2.3 %copy-start.6 = (bf16[64,256]{1,0:T(8,128)(2,1)S(1)}, bf16[64,256]{1,0:T(8,128)(2,1)}, u32[]{:S(2)}) copy-start(bf16[64,256]{1,0:T(8,128)(2,1)} %w_out.1) | copy-start | bytes 98308
  36.7 9.1 %collective-permute-start.14 = (bf16[512,128]{1,0:T(8,128)(2,1)S(1)}, bf16[512,128]{1,0:T(8,128)(2,1)S(1)}, u32[]{:S(2)}, u32[]{:S(2)}) collective-permute-start(bf16[512,128]{1,0:T(8,128)(2,1)S(1)} %get-tuple-element.44), channel_id=1, source_target_pairs={{1,0},{0,1},{3,2},{2,3},{5,4},{4,5},{7,6},{6,7},{9,8},{8,9},{11,10... | collective-permute-start | bytes 393224 | tf_op jit(solution)/shard_map/ppermute | solution.py:626
  40.0 11.4 %collective-permute-start.4 = (bf16[512,128]{1,0:T(8,128)(2,1)S(1)}, bf16[512,128]{1,0:T(8,128)(2,1)S(1)}, u32[]{:S(2)}, u32[]{:S(2)}) collective-permute-start(bf16[512,128]{1,0:T(8,128)(2,1)S(1)} %get-tuple-element.35), channel_id=1, source_target_pairs={{8,0},{9,1},{10,2},{11,3},{12,4},{13,5},{14,6},{15,7},{0,8},{1,9},... | collective-permute-start | bytes 393224 | tf_op jit(solution)/shard_map/ppermute | solution.py:626
  41.6 12.9 %collective-permute-start.5 = (bf16[512,128]{1,0:T(8,128)(2,1)S(1)}, bf16[512,128]{1,0:T(8,128)(2,1)S(1)}, u32[]{:S(2)}, u32[]{:S(2)}) collective-permute-start(bf16[512,128]{1,0:T(8,128)(2,1)S(1)} %get-tuple-element.36), channel_id=1, source_target_pairs={{16,0},{17,1},{18,2},{19,3},{20,4},{21,5},{22,6},{23,7},{24,8},{25... | collective-permute-start | bytes 393224 | tf_op jit(solution)/shard_map/ppermute | solution.py:626
  44.2 10.3 %collective-permute-start.6 = (bf16[512,128]{1,0:T(8,128)(2,1)S(1)}, bf16[512,128]{1,0:T(8,128)(2,1)S(1)}, u32[]{:S(2)}, u32[]{:S(2)}) collective-permute-start(bf16[512,128]{1,0:T(8,128)(2,1)S(1)} %get-tuple-element.37), channel_id=1, source_target_pairs={{24,0},{25,1},{26,2},{27,3},{28,4},{29,5},{30,6},{31,7},{16,8},{17... | collective-permute-start | bytes 393224 | tf_op jit(solution)/shard_map/ppermute | solution.py:626
  45.2 5.0 %collective-permute-start.16 = (bf16[512,128]{1,0:T(8,128)(2,1)S(1)}, bf16[512,128]{1,0:T(8,128)(2,1)S(1)}, u32[]{:S(2)}, u32[]{:S(2)}) collective-permute-start(bf16[512,128]{1,0:T(8,128)(2,1)S(1)} %get-tuple-element.47), channel_id=1, source_target_pairs={{1,0},{0,1},{3,2},{2,3},{5,4},{4,5},{7,6},{6,7},{9,8},{8,9},{11,10... | collective-permute-start | bytes 393224 | tf_op jit(solution)/shard_map/ppermute | solution.py:626
  45.8 9.7 %collective-permute-start.15 = (bf16[512,128]{1,0:T(8,128)(2,1)S(1)}, bf16[512,128]{1,0:T(8,128)(2,1)S(1)}, u32[]{:S(2)}, u32[]{:S(2)}) collective-permute-start(bf16[512,128]{1,0:T(8,128)(2,1)S(1)} %add_convert_fusion.1.refs_0_), channel_id=1, source_target_pairs={{8,0},{9,1},{10,2},{11,3},{12,4},{13,5},{14,6},{15,7},{0,8},{1,9},... | collective-permute-start | bytes 393224 | tf_op jit(solution)/shard_map/ppermute | solution.py:626
  50.2 0.8 %copy-start.7 = (bf16[128,128]{1,0:T(8,128)(2,1)S(1)}, bf16[128,128]{1,0:T(8,128)(2,1)}, u32[]{:S(2)}) copy-start(bf16[128,128]{1,0:T(8,128)(2,1)} %close_w.1) | copy-start | bytes 98308
  50.2 4.3 %copy-start = (bf16[32,32,256]{2,1,0:T(8,128)(2,1)S(1)}, bf16[32,32,256]{2,1,0:T(8,128)(2,1)}, u32[]{:S(2)}) copy-start(bf16[32,32,256]{2,1,0:T(8,128)(2,1)} %param.15) | copy-start | bytes 1572868
  50.3 6.8 %collective-permute-start.17 = (bf16[512,128]{1,0:T(8,128)(2,1)S(1)}, bf16[512,128]{1,0:T(8,128)(2,1)S(1)}, u32[]{:S(2)}, u32[]{:S(2)}) collective-permute-start(bf16[512,128]{1,0:T(8,128)(2,1)S(1)} %add_convert_fusion.refs_1_), channel_id=1, source_target_pairs={{8,0},{9,1},{10,2},{11,3},{12,4},{13,5},{14,6},{15,7},{0,8},{1,9},... | collective-permute-start | bytes 393224 | tf_op jit(solution)/shard_map/ppermute | solution.py:626
  54.5 0.9 %copy-start.1 = (bf16[128,128]{1,0:T(8,128)(2,1)S(1)}, bf16[128,128]{1,0:T(8,128)(2,1)}, u32[]{:S(2)}) copy-start(bf16[128,128]{1,0:T(8,128)(2,1)} %refs_5_.1) | copy-start | bytes 98308
